TPU v7x, 256 devices: a whole 4x4x8 slice. The times are simulated.
256 devices in a mesh: band: 64 (over x, z_hi, y), lev: 4 (over z_lo, core).
Axes of the slice: x: 4, y: 4, z: 8 (z_hi: 4, z_lo: 2; z = z_hi * 2 + z_lo), core: 2. Of those that a mesh axis runs over, the one named last changes fastest.
Arguments:
- pattern: float32 [8192, 128], P('band'), may hold values from -3 to 3
- taper: float32 [136], P('lev'), may hold values from 0.1 to 1
- thickness: float32 [136], P('lev'), may hold values from 0.2 to 2
- block_source: int32 [8192], P('band'), may hold values from 0 to 8191, as said below
- tendencies: bfloat16 [4, 136, 1048576], P(None, 'lev', 'band'), may hold values from -6 to 6
Outputs:
- perturbed: bfloat16 [4, 136, 1048576], P(None, 'lev', 'band')
- integrals: float32 [2, 1048576], P(None, 'band')
Inputs may be any that keep to these rules, and one draw needn't show every extreme that they name: block_source is a permutation of 0 to 8191; the 128 physics blocks of each band index take exactly 128 // 64 grid blocks from the 128 grid blocks of each band index.
All inputs are finite; a program needn't handle non-finite values.
Results may differ from a plain program's by a relative error of at most 0.001.
Values sent between devices are 32-bit elements; how exact they have to be, the bound alone decides.
No kernel may reach another device: no remote copies, remote signals or barrier semaphores. Data moves between devices by JAX's collectives and lax.ppermute only.
A program may use at most 64 MiB of HBM per device.

v0:
```python
import jax
import jax.numpy as jnp
from jax import lax
from jax.sharding import PartitionSpec as P


def laid_out(blocks, dim):
    lengths = list(blocks.shape[1:])
    lengths[dim] *= blocks.shape[0]
    return jnp.moveaxis(blocks, 0, dim).reshape(lengths)


def sent_to_all(x, axis):
    count = lax.axis_size(axis)
    return lax.all_to_all(jnp.broadcast_to(x[None], (count, *x.shape)), axis, 0, 0, tiled=True)


def collect(x, axis, dim):
    return laid_out(sent_to_all(x, axis), dim)


def taken_together(x, axis):
    return sent_to_all(x, axis).sum(axis=0)


def packed_total(arrays, axis):
    ends = [0]
    for a in arrays:
        ends.append(ends[-1] + a.size)
    subtotal = taken_together(jnp.concatenate([a.ravel() for a in arrays]), axis)
    return tuple((subtotal[b:e].reshape(a.shape) for a, b, e in zip(arrays, ends, ends[1:])))


def outgoing_blocks(clipped, block_source):
    blocks = clipped.shape[0]
    all_sources = collect(block_source, "band", 0)
    positions = jnp.argsort(all_sources)
    start = lax.axis_index("band") * blocks
    mine = lax.dynamic_slice_in_dim(positions, start, blocks, 0)
    owners = mine // blocks
    send_order = jnp.argsort(owners, stable=True)
    return jnp.take(clipped, send_order, axis=0)


def body(pattern, taper, thickness, block_source, tendencies):
    clipped = jnp.tanh(pattern)
    arrival_order = jnp.argsort(block_source)
    placing = jnp.argsort(arrival_order)
    outgoing = outgoing_blocks(clipped, block_source)
    arrived = lax.all_to_all(outgoing, "band", split_axis=0, concat_axis=0, tiled=True)
    local = jnp.take(arrived, placing, axis=0).reshape(-1)
    pert = taper[:, None] * local[None, :]
    perturbed = (tendencies.astype(jnp.float32) * (1.0 + pert)[None, :, :]).astype(jnp.bfloat16)
    moist = tendencies[2:4].astype(jnp.float32)
    partial_sums = jnp.sum(thickness[None, :, None] * moist * pert[None, :, :], axis=1)
    column_total, squares = packed_total((partial_sums, jnp.sum(thickness * thickness)), "lev")
    integrals = column_total / jnp.sqrt(squares)
    return (perturbed, integrals)


def solution(mesh):
    in_specs = (P("band", None), P("lev"), P("lev"), P("band"), P(None, "lev", "band"))
    out_specs = (P(None, "lev", "band"), P(None, "band"))
    return jax.shard_map(body, mesh=mesh, in_specs=in_specs, out_specs=out_specs, check_vma=False)
```

profile of v0, /device:TPU:1, one launch (start us, length us, event | category | flops | bytes accessed | tf_op | source)
XLA Modules:
  0.0 83.2 jit_solution(8171781289312810082)
XLA Ops:
  0.6 0.0 copy-start.1
  0.6 1.3 %broadcast_in_dim.13 = s32[64,1,128]{2,1,0:T(1,128)} broadcast(s32[128]{0:T(128)} %param.10), dimensions={2} | broadcast | bytes 33280 | tf_op jit(solution)/shard_map/broadcast_in_dim | solution.py:15
  1.9 15.1 %all-to-all-start = ((s32[64,1,128]{2,1,0:T(1,128)}), s32[64,1,128]{2,1,0:T(1,128)S(1)}, u32[]{:S(2)}, u32[]{:S(2)}) async-start(s32[64,1,128]{2,1,0:T(1,128)} %broadcast_in_dim.13), calls=%async_computation | async-start | bytes 65536 | tf_op jit(solution)/shard_map/all_to_all | solution.py:15
  17.1 3.2 %sort.67 = (s32[128]{0:T(128)}, s32[128]{0:T(128)S(1)}) sort(s32[128]{0:T(128)} %param.10, s32[128]{0:T(128)S(1)} %iota.17), dimensions={0}, to_apply=%region_2.4 | sort | flops 896 | bytes 2048 | tf_op jit(solution)/shard_map/jit(argsort)/sort | solution.py:47
  20.2 2.5 %sort.68 = (s32[128]{0:T(128)}, s32[128]{0:T(128)S(1)}) sort(s32[128]{0:T(128)S(1)} %get-tuple-element.9, s32[128]{0:T(128)S(1)} %iota.18), dimensions={0}, to_apply=%region_3.5 | sort | flops 896 | bytes 2048 | tf_op jit(solution)/shard_map/jit(argsort)/sort | solution.py:48
  22.8 0.9 %tanh.3 = f32[128,128]{1,0:T(8,128)S(1)} tanh(f32[128,128]{1,0:T(8,128)} %param.7) | non-fusion elementwise | bytes 131072 | tf_op jit(solution)/shard_map/tanh | solution.py:46
  23.7 4.1 %all-to-all-done = s32[64,1,128]{2,1,0:T(1,128)S(1)} async-done(((s32[64,1,128]{2,1,0:T(1,128)}), s32[64,1,128]{2,1,0:T(1,128)S(1)}, u32[]{:S(2)}, u32[]{:S(2)}) %all-to-all-start) | async-done | bytes 32800 | tf_op jit(solution)/shard_map/all_to_all | solution.py:15
  27.8 6.8 %sort.65 = (s32[8192]{0:T(1024)}, s32[8192]{0:T(1024)S(1)}) sort(s32[8192]{0:T(1024)S(1)} %bitcast.12, s32[8192]{0:T(1024)S(1)} %iota.15), dimensions={0}, to_apply=%region_0.0 | sort | flops 106496 | bytes 131072 | tf_op jit(solution)/shard_map/jit(argsort)/sort | solution.py:37
  34.6 0.1 and_select_fusion
  34.7 2.5 %sort.66 = (s32[128]{0:T(128)}, s32[128]{0:T(128)S(1)}) sort(s32[128]{0:T(128)S(1)} %and_select_fusion, s32[128]{0:T(128)S(1)} %iota.16), dimensions={0}, to_apply=%region_1.2 | sort | flops 896 | bytes 2048 | tf_op jit(solution)/shard_map/jit(argsort)/sort | solution.py:41
  37.2 0.6 gather_fusion
  37.9 0.7 broadcast_select_fusion
  38.6 8.0 %all-to-all-start.1 = ((f32[64,2,128]{2,1,0:T(2,128)}), f32[64,2,128]{2,1,0:T(2,128)S(1)}, u32[]{:S(2)}, u32[]{:S(2)}) async-start(f32[64,2,128]{2,1,0:T(2,128)} %bitcast.1), calls=%async_computation.1 | async-start | bytes 131072 | tf_op jit(solution)/shard_map/all_to_all | solution.py:50
  46.6 1.3 %multiply_reduce_fusion.1 = f32[]{:T(128)} fusion(f32[34]{0:T(128)} %param.9), kind=kLoop, calls=%fused_computation.20 | loop fusion | flops 67 | bytes 140 | tf_op jit(solution)/shard_map/reduce_sum | solution.py:56
  47.9 9.7 %all-to-all-done.1 = f32[64,2,128]{2,1,0:T(2,128)S(1)} async-done(((f32[64,2,128]{2,1,0:T(2,128)}), f32[64,2,128]{2,1,0:T(2,128)S(1)}, u32[]{:S(2)}, u32[]{:S(2)}) %all-to-all-start.1) | async-done | bytes 65568 | tf_op jit(solution)/shard_map/all_to_all | solution.py:50
  57.6 0.6 gather_fusion.1
  58.3 0.0 copy-start
  58.3 0.1 select_bitcast_fusion
  58.4 1.2 %broadcast_multiply_fusion = (f32[34,16384]{1,0:T(8,128)S(1)}, f32[34,16384]{1,0:T(8,128)S(1)}) fusion(f32[16384]{0:T(1024)S(1)} %select_bitcast_fusion, f32[34]{0:T(128)} %param.8), kind=kLoop, calls=%fused_computation.5 | loop fusion | flops 1114112 | bytes 4522120 | tf_op jit(solution)/shard_map/mul | solution.py:52
  59.6 0.0 copy-done.1
  59.6 1.0 %copy-done = bf16[4,34,16384]{2,0,1:T(4,128)(2,1)S(1)} copy-done((bf16[4,34,16384]{2,0,1:T(4,128)(2,1)S(1)}, bf16[4,34,16384]{2,0,1:T(4,128)(2,1)}, u32[]{:S(2)}) %copy-start) | copy-done | bytes 4456472
  60.6 4.5 %multiply_reduce_fusion = f32[2,16384]{1,0:T(2,128)S(1)} fusion(f32[34]{0:T(128)S(1)} %copy-done.1, f32[34,16384]{1,0:T(8,128)S(1)} %get-tuple-element.11, bf16[4,34,16384]{2,0,1:T(4,128)(2,1)S(1)} %copy-done), kind=kLoop, calls=%fused_computation.3 | loop fusion | flops 4423680 | bytes 4587656 | tf_op jit(solution)/shard_map/reduce_sum | solution.py:55
  65.0 0.7 pad_maximum_fusion
  65.7 1.1 %broadcast_in_dim.14 = f32[4,1,32769]{2,1,0:T(1,128)} broadcast(f32[32769]{0:T(1024)S(1)} %pad_maximum_fusion), dimensions={2} | broadcast | bytes 655380 | tf_op jit(solution)/shard_map/broadcast_in_dim | solution.py:15
  66.8 6.1 %all-to-all-start.2 = ((f32[4,1,32769]{2,1,0:T(1,128)}), f32[4,1,32769]{2,1,0:T(1,128)S(1)}, u32[]{:S(2)}, u32[]{:S(2)}) async-start(f32[4,1,32769]{2,1,0:T(1,128)} %broadcast_in_dim.14), calls=%async_computation.2 | async-start | bytes 1052672 | tf_op jit(solution)/shard_map/all_to_all | solution.py:15
  72.9 7.8 %multiply_convert_fusion = bf16[4,34,16384]{2,0,1:T(4,128)(2,1)} fusion(bf16[4,34,16384]{2,0,1:T(4,128)(2,1)} %param.11, f32[34,16384]{1,0:T(8,128)S(1)} %get-tuple-element.12), kind=kLoop, calls=%fused_computation.2 | loop fusion | flops 6684672 | bytes 11141120 | tf_op jit(solution)/shard_map/convert_element_type | solution.py:53
  80.7 0.1 all-to-all-done.2
  80.7 0.5 reduce_sum.29
  81.2 0.5 slice.17
  82.5 0.7 div.27
  (12 shorter events, 0.1 us)
Async XLA Ops:
  0.6 59.0 %copy-start.1 = (f32[34]{0:T(128)S(1)}, f32[34]{0:T(128)}, u32[]{:S(2)}) copy-start(f32[34]{0:T(128)} %param.9) | copy-start | bytes 412
  1.9 25.9 %all-to-all-start = ((s32[64,1,128]{2,1,0:T(1,128)}), s32[64,1,128]{2,1,0:T(1,128)S(1)}, u32[]{:S(2)}, u32[]{:S(2)}) async-start(s32[64,1,128]{2,1,0:T(1,128)} %broadcast_in_dim.13), calls=%async_computation | async-start | bytes 65536 | tf_op jit(solution)/shard_map/all_to_all | solution.py:15
  38.6 19.1 %all-to-all-start.1 = ((f32[64,2,128]{2,1,0:T(2,128)}), f32[64,2,128]{2,1,0:T(2,128)S(1)}, u32[]{:S(2)}, u32[]{:S(2)}) async-start(f32[64,2,128]{2,1,0:T(2,128)} %bitcast.1), calls=%async_computation.1 | async-start | bytes 131072 | tf_op jit(solution)/shard_map/all_to_all | solution.py:50
  58.3 2.3 %copy-start = (bf16[4,34,16384]{2,0,1:T(4,128)(2,1)S(1)}, bf16[4,34,16384]{2,0,1:T(4,128)(2,1)}, u32[]{:S(2)}) copy-start(bf16[4,34,16384]{2,0,1:T(4,128)(2,1)} %param.11) | copy-start | bytes 13369348
  66.8 14.0 %all-to-all-start.2 = ((f32[4,1,32769]{2,1,0:T(1,128)}), f32[4,1,32769]{2,1,0:T(1,128)S(1)}, u32[]{:S(2)}, u32[]{:S(2)}) async-start(f32[4,1,32769]{2,1,0:T(1,128)} %broadcast_in_dim.14), calls=%async_computation.2 | async-start | bytes 1052672 | tf_op jit(solution)/shard_map/all_to_all | solution.py:15
where the time goes:
time: 83.6 us; the launch traced here: 83.2 us
  other arithmetic  31.9 us (38%)
  starting transfers between devices  29.3 us (35%)
  waiting for transfers between devices  13.9 us (17%)
  local copies, waits for them, and re-layouts  6.73 us (8%)
  between operations  1.44 us (2%)
    all_to_all x2, starting transfers between devices, sent_to_all(): lax.all_to_all(jnp.broadcast_to(x[None], (count, *x.shape)), axis, 0, 0,...  21.2 us
    all_to_all x1, waiting for transfers between devices, body(): lax.all_to_all(outgoing, 'band', split_axis=0, concat_axis=0, tiled=True)  9.72 us
    all_to_all x1, starting transfers between devices, body(): lax.all_to_all(outgoing, 'band', split_axis=0, concat_axis=0, tiled=True)  8.05 us
    convert_element_type x1, other arithmetic, body(): (tendencies.astype(jnp.float32) * (1.0 + pert)[None, :, :]).astype(jnp.bf...  7.81 us
    sort x1, other arithmetic, outgoing_blocks(): positions = jnp.argsort(all_sources)  6.77 us
    reduce_sum x1, other arithmetic, body(): jnp.sum(thickness[None, :, None] * moist * pert[None, :, :], axis=1)  4.45 us
    all_to_all x2, waiting for transfers between devices, sent_to_all(): lax.all_to_all(jnp.broadcast_to(x[None], (count, *x.shape)), axis, 0, 0,...  4.2 us
    sort x1, other arithmetic, body(): arrival_order = jnp.argsort(block_source)  3.19 us
  transfers between devices with their start and end apart: 3, of which 3 were waited for; matrix products, arithmetic and copies ran while one was open for 19% of the time, Pallas kernels for 0%

commit v1 on v0

v1 whole, which is shorter than its diff:
```python
import functools

import jax
import jax.numpy as jnp
from jax import lax
from jax.experimental import pallas as pl
from jax.experimental.pallas import tpu as pltpu
from jax.sharding import PartitionSpec as P

PLANE = [[x * 16 + z * 4 + y for x in range(4) for y in range(4)] for z in range(4)]
ROW = 128


def onto(band, step):
    return (band // 16) * 16 + ((band // 4 + step) % 4) * 4 + band % 4


def along_z(a, step):
    return lax.ppermute(a, "band", [(b, onto(b, step)) for b in range(64)])


def across_lev(a, flip):
    return lax.ppermute(a, "lev", [(i, i ^ flip) for i in range(4)])


def within_plane(a):
    return lax.all_to_all(a, "band", 0, 0, tiled=True, axis_index_groups=PLANE)


def iota(shape, dim):
    return lax.broadcasted_iota(jnp.int32, shape, dim)


def onehot(cond):
    return jnp.where(cond, 1.0, 0.0).astype(jnp.bfloat16)


def dot(a, b):
    return jnp.dot(a, b, preferred_element_type=jnp.float32)


def dot_nt(a, b):
    return lax.dot_general(a, b, (((1,), (1,)), ((), ())), preferred_element_type=jnp.float32)


def three_parts(v):
    high = v.astype(jnp.bfloat16)
    rest = v - high.astype(jnp.float32)
    mid = rest.astype(jnp.bfloat16)
    low = (rest - mid.astype(jnp.float32)).astype(jnp.bfloat16)
    return high, mid, low


def request_kernel(source_ref, ids_ref, pos_ref):
    source = source_ref[...]
    band, row = source >> 7, source & 127
    group = (band >> 4) * 4 + (band & 3)
    my_z = (lax.axis_index("band") >> 2) & 3
    table = (my_z - ((band >> 2) & 3)) & 3
    member = iota((16, ROW), 0) == group
    before = onehot(iota((ROW, ROW), 0) < iota((ROW, ROW), 1))
    count = dot(onehot(member), before)
    rank = jnp.sum(jnp.where(member, count, 0.0), axis=0, keepdims=True)
    pos = group * 8 + rank.astype(jnp.int32)
    slot = onehot(iota((ROW, ROW), 0) == pos)

    def everywhere(v):
        return jnp.broadcast_to(v.astype(jnp.float32), (ROW, ROW)).astype(jnp.bfloat16)

    ids = dot_nt(slot, everywhere(table)) * 128.0 + dot_nt(slot, everywhere(row))
    ids_ref[...] = ids.astype(jnp.int32)
    pos_ref[...] = jnp.broadcast_to(pos, pos_ref.shape)


def pick_kernel(ids_ref, t0, t1, t2, t3, out_ref):
    ids = ids_ref[...]
    lane = iota((ROW, ROW), 1)
    total = None
    for c, ref in enumerate((t0, t1, t2, t3)):
        pick = onehot(ids == lane + c * ROW)
        high, mid, low = three_parts(ref[...])
        part = (dot(pick, high), dot(pick, mid), dot(pick, low))
        total = part if total is None else tuple(a + b for a, b in zip(total, part))
    out_ref[...] = (total[0] + total[1]) + total[2]


def column_kernel(taper_ref, thick_ref, pos_ref, x_ref, sums_ref, place_ref, acc_ref):
    levels = x_ref.shape[0]
    pos = jnp.broadcast_to(pos_ref[0:1, :].astype(jnp.float32), (ROW, ROW)).astype(jnp.bfloat16)
    expand = onehot(iota((4 * ROW, ROW), 0) >> 2 == iota((4 * ROW, ROW), 1))
    slot = dot_nt(expand, pos).astype(jnp.int32)
    place_ref[...] = onehot(slot == iota((4 * ROW, ROW), 1))

    weights = [taper_ref[l] * thick_ref[l] for l in range(levels)]

    def chunk(i, carry):
        rows = pl.ds(pl.multiple_of(i * 64, 64), 64)
        acc = x_ref[0, rows, :].astype(jnp.float32) * weights[0]
        for l in range(1, levels):
            acc = acc + x_ref[l, rows, :].astype(jnp.float32) * weights[l]
        acc_ref[rows, :] = acc
        return carry

    lax.fori_loop(0, 8, chunk, 0)
    for k in range(2):
        sums_ref[pl.ds(k * ROW, ROW), :] = acc_ref[pl.ds(2 + k, ROW, stride=4), :]
    squares = thick_ref[0] * thick_ref[0]
    for l in range(1, levels):
        squares = squares + thick_ref[l] * thick_ref[l]
    sums_ref[pl.ds(2 * ROW, 8), :] = jnp.full((8, ROW), squares, jnp.float32)


def perturb_kernel(taper_ref, arrived_ref, place_ref, s0, s1, s2, s3, x_ref, y_ref, out_ref, local_ref):
    levels = x_ref.shape[0]
    step = pl.program_id(0)

    @pl.when(step == 0)
    def _():
        parts = three_parts(jnp.tanh(arrived_ref[...]))
        place = place_ref[...]
        local_ref[...] = (dot(place, parts[0]) + dot(place, parts[1])) + dot(place, parts[2])
        total = (s0[...] + s1[...]) + (s2[...] + s3[...])
        norm = jnp.sqrt(total[2 * ROW : 2 * ROW + 1, :])
        local = local_ref[pl.ds(0, ROW, stride=4), :]
        for k in range(2):
            out_ref[pl.ds(k, ROW, stride=2), :] = local * total[k * ROW : (k + 1) * ROW, :] / norm

    rows = x_ref.shape[1]
    for r in range(0, rows, 32):
        local = local_ref[pl.ds(pl.multiple_of(step * rows + r, 32), 32), :]
        for l in range(levels):
            scale = 1.0 + taper_ref[l] * local
            y_ref[l, r : r + 32, :] = (x_ref[l, r : r + 32, :].astype(jnp.float32) * scale).astype(jnp.bfloat16)


def body(pattern, taper, thickness, block_source, tendencies):
    vmem, smem = pl.BlockSpec(memory_space=pltpu.VMEM), pl.BlockSpec(memory_space=pltpu.SMEM)
    levels = tendencies.shape[1]
    f32, s32 = jnp.float32, jnp.int32

    tables = [pattern] + [along_z(pattern, k) for k in (1, 2, 3)]
    ids, pos = pl.pallas_call(
        request_kernel,
        out_shape=(jax.ShapeDtypeStruct((ROW, ROW), s32), jax.ShapeDtypeStruct((8, ROW), s32)),
        in_specs=[vmem],
        out_specs=(vmem, vmem),
        compiler_params=pltpu.CompilerParams(vmem_limit_bytes=4 << 20),
        name="request",
    )(block_source.reshape(1, ROW))
    wanted = within_plane(ids.reshape(16, 8, ROW)).reshape(ROW, ROW)

    x = tendencies.reshape(4, levels, ROW, ROW).transpose(1, 2, 0, 3).reshape(levels, 4 * ROW, ROW)
    sums, place = pl.pallas_call(
        column_kernel,
        out_shape=(jax.ShapeDtypeStruct((2 * ROW + 8, ROW), f32), jax.ShapeDtypeStruct((4 * ROW, ROW), jnp.bfloat16)),
        in_specs=[smem, smem, vmem, vmem],
        out_specs=(vmem, vmem),
        scratch_shapes=[pltpu.VMEM((4 * ROW, ROW), f32)],
        cost_estimate=pl.CostEstimate(flops=10_000_000, bytes_accessed=4_500_000, transcendentals=0),
        compiler_params=pltpu.CompilerParams(vmem_limit_bytes=12 << 20),
        name="columns",
    )(taper, thickness, pos, x)
    others = [across_lev(sums, flip) for flip in (1, 2, 3)]

    picked = pl.pallas_call(
        pick_kernel,
        out_shape=jax.ShapeDtypeStruct((ROW, ROW), f32),
        in_specs=[vmem] * 5,
        out_specs=vmem,
        compiler_params=pltpu.CompilerParams(vmem_limit_bytes=4 << 20),
        name="pick",
    )(wanted, *tables)
    arrived = within_plane(picked.reshape(16, 8, ROW)).reshape(ROW, ROW)

    steps = 8
    rows = 4 * ROW // steps
    whole = lambda shape: pl.BlockSpec(shape, lambda i: (0,) * len(shape))
    stream = pl.BlockSpec((levels, rows, ROW), lambda i: (0, i, 0))
    y, out = pl.pallas_call(
        perturb_kernel,
        grid=(steps,),
        out_shape=(jax.ShapeDtypeStruct(x.shape, x.dtype), jax.ShapeDtypeStruct((2 * ROW, ROW), f32)),
        in_specs=[smem, whole((ROW, ROW)), whole((4 * ROW, ROW))] + [whole(sums.shape)] * 4 + [stream],
        out_specs=(stream, whole((2 * ROW, ROW))),
        scratch_shapes=[pltpu.VMEM((4 * ROW, ROW), f32)],
        cost_estimate=pl.CostEstimate(flops=10_000_000, bytes_accessed=9_000_000, transcendentals=0),
        compiler_params=pltpu.CompilerParams(vmem_limit_bytes=12 << 20),
        name="perturb",
    )(taper, arrived, place, sums, *others, x)
    perturbed = y.reshape(levels, ROW, 4, ROW).transpose(2, 0, 1, 3).reshape(tendencies.shape)
    integrals = out.reshape(ROW, 2, ROW).transpose(1, 0, 2).reshape(2, ROW * ROW)
    return perturbed, integrals


def solution(mesh):
    in_specs = (P("band", None), P("lev"), P("lev"), P("band"), P(None, "lev", "band"))
    out_specs = (P(None, "lev", "band"), P(None, "band"))
    return jax.shard_map(body, mesh=mesh, in_specs=in_specs, out_specs=out_specs, check_vma=False)
```

time: 83.6 us -> 50.7 us (0.61)
  the two profiles are of different devices: /device:TPU:1 before, /device:TPU:32 now
where the time goes in v1:
time: 50.7 us; the launch traced here: 50.5 us
  blocking collectives  25.4 us (50%)
  starting transfers between devices  12.5 us (25%)
  Pallas kernels  7.67 us (15%)
  local copies, waits for them, and re-layouts  4.24 us (8%)
  between operations  0.7 us (1%)
    all_to_all x2, blocking collectives, within_plane(): return lax.all_to_all(a, 'band', 0, 0, tiled=True, axis_index_groups=PLANE)  25.4 us
    ppermute x3, starting transfers between devices, along_z(): return lax.ppermute(a, 'band', [(b, onto(b, step)) for b in range(64)])  10.5 us
    pallas_call x1, Pallas kernels, body(): pl.pallas_call(perturb_kernel, grid=(steps,), out_shape=(jax.ShapeDtypeSt...  5.22 us
    unnamed x14, local copies, waits for them, and re-layouts  4.24 us
    ppermute x3, starting transfers between devices, across_lev(): return lax.ppermute(a, 'lev', [(i, i ^ flip) for i in range(4)])  1.95 us
    pallas_call x1, Pallas kernels, body(): pl.pallas_call(column_kernel, out_shape=(jax.ShapeDtypeStruct((2 * ROW +...  1.91 us
  transfers between devices with their start and end apart: 6, of which 0 were waited for; matrix products, arithmetic and copies ran while one was open for 0% of the time, Pallas kernels for 5%

profile of v1, /device:TPU:32, one launch (start us, length us, event | category | flops | bytes accessed | tf_op | source)
XLA Modules:
  0.0 50.5 jit_solution(14808428999160178597)
XLA Ops:
  0.6 0.0 copy-start.4
  0.6 6.4 %collective-permute-start.1 = (f32[128,128]{1,0:T(8,128)}, f32[128,128]{1,0:T(8,128)S(1)}, u32[]{:S(2)}, u32[]{:S(2)}) collective-permute-start(f32[128,128]{1,0:T(8,128)} %t0.1), channel_id=1, source_target_pairs={{0,32},{4,36},{8,40},{12,44},{16,48},{20,52},{24,56},{28,60},{32,0... | collective-permute-start | bytes 196616 | tf_op jit(solution)/shard_map/ppermute | solution.py:19
  7.0 0.0 copy-start.6
  7.0 0.7 %copy-done.6 = s32[128]{0:T(128)S(1)} copy-done((s32[128]{0:T(128)S(1)}, s32[128]{0:T(128)}, u32[]{:S(2)}) %copy-start.6) | copy-done | bytes 536
  7.7 0.3 request.1
  8.0 0.0 copy-start
  8.0 2.3 %copy-done = bf16[4,34,16384]{2,0,1:T(4,128)(2,1)S(1)} copy-done((bf16[4,34,16384]{2,0,1:T(4,128)(2,1)S(1)}, bf16[4,34,16384]{2,0,1:T(4,128)(2,1)}, u32[]{:S(2)}) %copy-start) | copy-done | bytes 4456472
  10.2 0.0 copy-start.3
  10.2 0.7 %copy-done.3 = f32[34]{0:T(128)S(1)} copy-done((f32[34]{0:T(128)S(1)}, f32[34]{0:T(128)}, u32[]{:S(2)}) %copy-start.3) | copy-done | bytes 160
  10.9 0.0 copy-start.5
  10.9 0.7 %copy-done.5 = f32[34]{0:T(128)S(1)} copy-done((f32[34]{0:T(128)S(1)}, f32[34]{0:T(128)}, u32[]{:S(2)}) %copy-start.5) | copy-done | bytes 160
  11.5 0.0 copy-start.2
  11.5 0.0 copy-start.1
  11.5 1.9 %columns.1 = (f32[264,128]{1,0:T(8,128)S(1)}, bf16[512,128]{1,0:T(8,128)(2,1)S(1)}) custom-call(f32[34]{0:T(128)S(1)} %copy-done.3, f32[34]{0:T(128)S(1)} %copy-done.5, s32[8,128]{1,0:T(8,128)S(1)} %get-tuple-element.9.pos_ref, bf16[34,512,128]{2,1,0:T(8,128)(2,1)S(1)} %bitcast.20), custom_call_target="tpu_custom_call" | custom-call | flops 10000000 | bytes 4500000 | tf_op jit(solution)/shard_map/columns/pallas_call | solution.py:153
  13.5 0.3 collective-permute-start.5
  13.7 1.0 %collective-permute-start.4 = (f32[264,128]{1,0:T(8,128)S(1)}, f32[264,128]{1,0:T(8,128)S(1)}, u32[]{:S(2)}, u32[]{:S(2)}) collective-permute-start(f32[264,128]{1,0:T(8,128)S(1)} %get-tuple-element.11.s0), channel_id=1, source_target_pairs={{0,2},{1,3},{2,0},{3,1},{4,6},{5,7},{6,4},{7,5},{8,10},{9,11},{10,... | collective-permute-start | bytes 405512 | tf_op jit(solution)/shard_map/ppermute | solution.py:23
  14.7 0.7 %collective-permute-start.3 = (f32[264,128]{1,0:T(8,128)S(1)}, f32[264,128]{1,0:T(8,128)S(1)}, u32[]{:S(2)}, u32[]{:S(2)}) collective-permute-start(f32[264,128]{1,0:T(8,128)S(1)} %get-tuple-element.11.s0), channel_id=1, source_target_pairs={{0,1},{1,0},{2,3},{3,2},{4,5},{5,4},{6,7},{7,6},{8,9},{9,8},{10,11... | collective-permute-start | bytes 405512 | tf_op jit(solution)/shard_map/ppermute | solution.py:23
  15.4 1.5 %collective-permute-start = (f32[128,128]{1,0:T(8,128)}, f32[128,128]{1,0:T(8,128)S(1)}, u32[]{:S(2)}, u32[]{:S(2)}) collective-permute-start(f32[128,128]{1,0:T(8,128)} %t0.1), channel_id=1, source_target_pairs={{0,16},{4,20},{8,24},{12,28},{16,32},{20,36},{24,40},{28,44},{32,4... | collective-permute-start | bytes 196616 | tf_op jit(solution)/shard_map/ppermute | solution.py:19
  16.9 0.0 collective-permute-done.1.t2
  16.9 2.7 %collective-permute-start.2 = (f32[128,128]{1,0:T(8,128)}, f32[128,128]{1,0:T(8,128)S(1)}, u32[]{:S(2)}, u32[]{:S(2)}) collective-permute-start(f32[128,128]{1,0:T(8,128)} %t0.1), channel_id=1, source_target_pairs={{0,48},{4,52},{8,56},{12,60},{16,0},{20,4},{24,8},{28,12},{32,16},... | collective-permute-start | bytes 196616 | tf_op jit(solution)/shard_map/ppermute | solution.py:19
  19.5 14.5 %all_to_all.10 = s32[16,8,128]{2,1,0:T(8,128)S(1)} all-to-all(s32[16,8,128]{2,1,0:T(8,128)S(1)} %bitcast.25), channel_id=1, replica_groups={{0,4,8,12,64,68,72,76,128,132,136,140,192,196,200,204},{16,20,24,28,80,..., dimensions={0} | all-to-all | bytes 131072 | tf_op jit(solution)/shard_map/all_to_all | solution.py:27
  34.0 0.0 collective-permute-done.t1
  34.0 0.0 collective-permute-done.2.t3
  34.0 0.0 copy-done.2
  34.0 0.3 pick.1
  34.3 10.9 %all_to_all.11 = f32[16,8,128]{2,1,0:T(8,128)S(1)} all-to-all(f32[16,8,128]{2,1,0:T(8,128)S(1)} %bitcast.24), channel_id=1, replica_groups={{0,4,8,12,64,68,72,76,128,132,136,140,192,196,200,204},{16,20,24,28,80,..., dimensions={0} | all-to-all | bytes 131072 | tf_op jit(solution)/shard_map/all_to_all | solution.py:27
  45.2 0.0 collective-permute-done.5.s3
  45.2 0.0 collective-permute-done.4.s2
  45.2 0.0 collective-permute-done.3.s1
  45.2 0.0 copy-done.4
  45.2 0.0 copy-done.1
  45.2 5.2 %perturb.1 = (bf16[34,512,128]{2,1,0:T(8,128)(2,1)}, f32[256,128]{1,0:T(8,128)}) custom-call(f32[34]{0:T(128)S(1)} %copy-done.4, f32[128,128]{1,0:T(8,128)S(1)} %bitcast.22, bf16[512,128]{1,0:T(8,128)(2,1)S(1)} %get-tuple-element.10.place_ref, f32[264,128]{1,0:T(8,128)S(1)} %get-tuple-element.11.s0, f32[264,128]{1,0:T(8,128)S(1)} %collective-permute-done.3.s1, ...), custom_call_target="tpu_custom_call" | custom-call | flops 10000000 | bytes 9000000 | tf_op jit(solution)/shard_map/perturb/pallas_call | solution.py:179
Async XLA Ops:
  0.6 44.6 %copy-start.4 = (f32[34]{0:T(128)S(1)}, f32[34]{0:T(128)}, u32[]{:S(2)}) copy-start(f32[34]{0:T(128)} %taper_ref.3) | copy-start | bytes 412
  0.6 16.2 %collective-permute-start.1 = (f32[128,128]{1,0:T(8,128)}, f32[128,128]{1,0:T(8,128)S(1)}, u32[]{:S(2)}, u32[]{:S(2)}) collective-permute-start(f32[128,128]{1,0:T(8,128)} %t0.1), channel_id=1, source_target_pairs={{0,32},{4,36},{8,40},{12,44},{16,48},{20,52},{24,56},{28,60},{32,0... | collective-permute-start | bytes 196616 | tf_op jit(solution)/shard_map/ppermute | solution.py:19
  7.0 0.7 %copy-start.6 = (s32[128]{0:T(128)S(1)}, s32[128]{0:T(128)}, u32[]{:S(2)}) copy-start(s32[128]{0:T(128)} %param.8) | copy-start | bytes 1540
  8.0 2.3 %copy-start = (bf16[4,34,16384]{2,0,1:T(4,128)(2,1)S(1)}, bf16[4,34,16384]{2,0,1:T(4,128)(2,1)}, u32[]{:S(2)}) copy-start(bf16[4,34,16384]{2,0,1:T(4,128)(2,1)} %param.9) | copy-start | bytes 13369348
  10.2 0.7 %copy-start.3 = (f32[34]{0:T(128)S(1)}, f32[34]{0:T(128)}, u32[]{:S(2)}) copy-start(f32[34]{0:T(128)} %taper_ref.3) | copy-start | bytes 412
  10.9 0.7 %copy-start.5 = (f32[34]{0:T(128)S(1)}, f32[34]{0:T(128)}, u32[]{:S(2)}) copy-start(f32[34]{0:T(128)} %thick_ref.1) | copy-start | bytes 412
  11.5 22.5 %copy-start.2 = (f32[128,128]{1,0:T(8,128)S(1)}, f32[128,128]{1,0:T(8,128)}, u32[]{:S(2)}) copy-start(f32[128,128]{1,0:T(8,128)} %t0.1) | copy-start | bytes 196612
  11.5 33.7 %copy-start.1 = (bf16[4,34,16384]{2,0,1:T(4,128)(2,1)S(1)}, bf16[4,34,16384]{2,0,1:T(4,128)(2,1)}, u32[]{:S(2)}) copy-start(bf16[4,34,16384]{2,0,1:T(4,128)(2,1)} %param.9) | copy-start | bytes 13369348
  13.5 31.8 %collective-permute-start.5 = (f32[264,128]{1,0:T(8,128)S(1)}, f32[264,128]{1,0:T(8,128)S(1)}, u32[]{:S(2)}, u32[]{:S(2)}) collective-permute-start(f32[264,128]{1,0:T(8,128)S(1)} %get-tuple-element.11.s0), channel_id=1, source_target_pairs={{0,3},{1,2},{2,1},{3,0},{4,7},{5,6},{6,5},{7,4},{8,11},{9,10},{10,... | collective-permute-start | bytes 405512 | tf_op jit(solution)/shard_map/ppermute | solution.py:23
  13.7 31.5 %collective-permute-start.4 = (f32[264,128]{1,0:T(8,128)S(1)}, f32[264,128]{1,0:T(8,128)S(1)}, u32[]{:S(2)}, u32[]{:S(2)}) collective-permute-start(f32[264,128]{1,0:T(8,128)S(1)} %get-tuple-element.11.s0), channel_id=1, source_target_pairs={{0,2},{1,3},{2,0},{3,1},{4,6},{5,7},{6,4},{7,5},{8,10},{9,11},{10,... | collective-permute-start | bytes 405512 | tf_op jit(solution)/shard_map/ppermute | solution.py:23
  14.7 30.5 %collective-permute-start.3 = (f32[264,128]{1,0:T(8,128)S(1)}, f32[264,128]{1,0:T(8,128)S(1)}, u32[]{:S(2)}, u32[]{:S(2)}) collective-permute-start(f32[264,128]{1,0:T(8,128)S(1)} %get-tuple-element.11.s0), channel_id=1, source_target_pairs={{0,1},{1,0},{2,3},{3,2},{4,5},{5,4},{6,7},{7,6},{8,9},{9,8},{10,11... | collective-permute-start | bytes 405512 | tf_op jit(solution)/shard_map/ppermute | solution.py:23
  15.4 18.6 %collective-permute-start = (f32[128,128]{1,0:T(8,128)}, f32[128,128]{1,0:T(8,128)S(1)}, u32[]{:S(2)}, u32[]{:S(2)}) collective-permute-start(f32[128,128]{1,0:T(8,128)} %t0.1), channel_id=1, source_target_pairs={{0,16},{4,20},{8,24},{12,28},{16,32},{20,36},{24,40},{28,44},{32,4... | collective-permute-start | bytes 196616 | tf_op jit(solution)/shard_map/ppermute | solution.py:19
  16.9 17.2 %collective-permute-start.2 = (f32[128,128]{1,0:T(8,128)}, f32[128,128]{1,0:T(8,128)S(1)}, u32[]{:S(2)}, u32[]{:S(2)}) collective-permute-start(f32[128,128]{1,0:T(8,128)} %t0.1), channel_id=1, source_target_pairs={{0,48},{4,52},{8,56},{12,60},{16,0},{20,4},{24,8},{28,12},{32,16},... | collective-permute-start | bytes 196616 | tf_op jit(solution)/shard_map/ppermute | solution.py:19

commit v2 on v1

v2 whole, which is shorter than its diff:
```python
import jax
import jax.numpy as jnp
from jax import lax
from jax.experimental import pallas as pl
from jax.experimental.pallas import tpu as pltpu
from jax.sharding import PartitionSpec as P


ROW = 128
LEVELS = 40
PARTS = 8
PART = 4 * ROW // PARTS


def along_z(a, step):
    return lax.ppermute(a, "z", [(i, (i + step) % 4) for i in range(4)])


def across_lev(a, flip):
    return lax.ppermute(a, "lev", [(i, i ^ flip) for i in range(4)])


def within_plane(a):
    return lax.all_to_all(a, ("x", "y"), 0, 0, tiled=True)


def iota(shape, dim):
    return lax.broadcasted_iota(jnp.int32, shape, dim)


def onehot(cond):
    return jnp.where(cond, 1.0, 0.0).astype(jnp.bfloat16)


def dot(a, b):
    return jnp.dot(a, b, preferred_element_type=jnp.float32)


def dot_nt(a, b):
    return lax.dot_general(a, b, (((1,), (1,)), ((), ())), preferred_element_type=jnp.float32)


def three_parts(v):
    high = v.astype(jnp.bfloat16)
    rest = v - high.astype(jnp.float32)
    mid = rest.astype(jnp.bfloat16)
    low = (rest - mid.astype(jnp.float32)).astype(jnp.bfloat16)
    return high, mid, low


def request_kernel(source_ref, taper_ref, thick_ref, ids_ref, pos_ref, scalars_ref):
    source = source_ref[...]
    band, row = source >> 7, source & 127
    group = (band >> 4) * 4 + (band & 3)
    my_z = lax.axis_index("z")
    table = (my_z - ((band >> 2) & 3)) & 3
    member = iota((16, ROW), 0) == group
    before = onehot(iota((ROW, ROW), 0) < iota((ROW, ROW), 1))
    count = dot(onehot(member), before)
    rank = jnp.sum(jnp.where(member, count, 0.0), axis=0, keepdims=True)
    pos = group * 8 + rank.astype(jnp.int32)
    slot = onehot(iota((ROW, ROW), 0) == pos)

    def everywhere(v):
        return jnp.broadcast_to(v.astype(jnp.float32), (ROW, ROW)).astype(jnp.bfloat16)

    ids = dot_nt(slot, everywhere(table)) * 128.0 + dot_nt(slot, everywhere(row))
    ids_ref[...] = ids.astype(jnp.int32)
    pos_ref[...] = jnp.broadcast_to(pos, pos_ref.shape)

    taper, thick = taper_ref[...], thick_ref[...]
    levels = taper.shape[1]
    diagonal = iota((LEVELS, levels), 0) == iota((LEVELS, levels), 1)

    def one_per_row(v):
        total = jnp.sum(jnp.where(diagonal, jnp.broadcast_to(v, diagonal.shape), 0.0), axis=1, keepdims=True)
        return jnp.broadcast_to(total, (LEVELS, ROW))

    scalars_ref[0:LEVELS, :] = one_per_row(taper)
    scalars_ref[LEVELS : 2 * LEVELS, :] = one_per_row(taper * thick)
    scalars_ref[2 * LEVELS :, :] = jnp.broadcast_to(jnp.sum(thick * thick, axis=1, keepdims=True), (8, ROW))


def pick_kernel(ids_ref, t0, t1, t2, t3, out_ref):
    ids = ids_ref[...]
    lane = iota((ROW, ROW), 1)
    total = None
    for c, ref in enumerate((t0, t1, t2, t3)):
        pick = onehot(ids == lane + c * ROW)
        high, mid, low = three_parts(ref[...])
        part = (dot(pick, high), dot(pick, mid), dot(pick, low))
        total = part if total is None else tuple(a + b for a, b in zip(total, part))
    out_ref[...] = (total[0] + total[1]) + total[2]


def fetches(x_hbm, x_ref, sems):
    def fetch(i):
        rows = pl.ds(pl.multiple_of(i * PART, PART), PART)
        return pltpu.make_async_copy(x_hbm.at[:, rows, :], x_ref.at[:, rows, :], sems.at[i])

    for i in range(PARTS):
        fetch(i).start()
    return fetch


def column_kernel(scalars_ref, pos_ref, x_hbm, sums_ref, place_ref, acc_ref, x_ref, sems):
    levels = x_ref.shape[0]
    fetch = fetches(x_hbm, x_ref, sems)
    pos = jnp.broadcast_to(pos_ref[0:1, :].astype(jnp.float32), (ROW, ROW)).astype(jnp.bfloat16)
    expand = onehot(iota((4 * ROW, ROW), 0) >> 2 == iota((4 * ROW, ROW), 1))
    slot = dot_nt(expand, pos).astype(jnp.int32)
    place_ref[...] = onehot(slot == iota((4 * ROW, ROW), 1))

    def chunk(i, carry):
        fetch(i).wait()
        for r in range(0, PART, 64):
            rows = pl.ds(pl.multiple_of(i * PART + r, 64), 64)
            acc = x_ref[0, rows, :].astype(jnp.float32) * scalars_ref[LEVELS : LEVELS + 1, :]
            for l in range(1, levels):
                acc = acc + x_ref[l, rows, :].astype(jnp.float32) * scalars_ref[LEVELS + l : LEVELS + l + 1, :]
            acc_ref[rows, :] = acc
        return carry

    lax.fori_loop(0, PARTS, chunk, 0)
    for k in range(2):
        sums_ref[pl.ds(k * ROW, ROW), :] = acc_ref[pl.ds(2 + k, ROW, stride=4), :]
    sums_ref[pl.ds(2 * ROW, 8), :] = scalars_ref[2 * LEVELS :, :]


def perturb_kernel(scalars_ref, arrived_ref, place_ref, x_hbm, y_hbm, clipped_ref, local_ref, x_ref, y_ref, in_sems, sems):
    levels = x_ref.shape[0]
    fetch = fetches(x_hbm, x_ref, in_sems)
    parts = three_parts(jnp.tanh(arrived_ref[...]))
    place = place_ref[...]
    local_ref[...] = (dot(place, parts[0]) + dot(place, parts[1])) + dot(place, parts[2])
    clipped_ref[...] = local_ref[pl.ds(0, ROW, stride=4), :]

    def store(i):
        rows = pl.ds(pl.multiple_of(i * PART, PART), PART)
        return pltpu.make_async_copy(y_ref.at[:, rows, :], y_hbm.at[:, rows, :], sems.at[i])

    def chunk(i, carry):
        fetch(i).wait()
        for r in range(0, PART, 32):
            rows = pl.ds(pl.multiple_of(i * PART + r, 32), 32)
            local = local_ref[rows, :]
            for l in range(levels):
                scale = 1.0 + scalars_ref[l : l + 1, :] * local
                y_ref[l, rows, :] = (x_ref[l, rows, :].astype(jnp.float32) * scale).astype(jnp.bfloat16)
        store(i).start()
        return carry

    lax.fori_loop(0, PARTS, chunk, 0)
    for i in range(PARTS):
        store(i).wait()


def integrals_kernel(local_ref, s0, s1, s2, s3, out_ref):
    local = local_ref[...]
    total = (s0[...] + s1[...]) + (s2[...] + s3[...])
    norm = jnp.sqrt(total[2 * ROW : 2 * ROW + 1, :])
    for k in range(2):
        out_ref[pl.ds(k, ROW, stride=2), :] = local * total[k * ROW : (k + 1) * ROW, :] / norm


def program(pattern, taper, thickness, block_source, tendencies):
    vmem, hbm = pl.BlockSpec(memory_space=pltpu.VMEM), pl.BlockSpec(memory_space=pltpu.HBM)
    levels = tendencies.shape[1]
    f32, s32 = jnp.float32, jnp.int32

    tables = [pattern] + [along_z(pattern, k) for k in (1, 2, 3)]
    scalar_rows = 2 * LEVELS + 8
    ids, pos, scalars = pl.pallas_call(
        request_kernel,
        out_shape=(
            jax.ShapeDtypeStruct((ROW, ROW), s32),
            jax.ShapeDtypeStruct((8, ROW), s32),
            jax.ShapeDtypeStruct((scalar_rows, ROW), f32),
        ),
        in_specs=[vmem, vmem, vmem],
        out_specs=(vmem, vmem, vmem),
        name="request",
    )(block_source.reshape(1, ROW), taper.reshape(1, levels), thickness.reshape(1, levels))
    wanted = within_plane(ids.reshape(16, 8, ROW)).reshape(ROW, ROW)

    x = tendencies.reshape(4, levels, ROW, ROW).transpose(1, 2, 0, 3).reshape(levels, 4 * ROW, ROW)
    sums, place = pl.pallas_call(
        column_kernel,
        out_shape=(jax.ShapeDtypeStruct((2 * ROW + 8, ROW), f32), jax.ShapeDtypeStruct((4 * ROW, ROW), jnp.bfloat16)),
        in_specs=[vmem, vmem, hbm],
        out_specs=(vmem, vmem),
        scratch_shapes=[
            pltpu.VMEM((4 * ROW, ROW), f32),
            pltpu.VMEM(x.shape, x.dtype),
            pltpu.SemaphoreType.DMA((PARTS,)),
        ],
        cost_estimate=pl.CostEstimate(flops=10_000_000, bytes_accessed=4_500_000, transcendentals=0),
        compiler_params=pltpu.CompilerParams(vmem_limit_bytes=52 << 20),
        name="columns",
    )(scalars, pos, x)
    others = [across_lev(sums, flip) for flip in (1, 2, 3)]

    picked = pl.pallas_call(
        pick_kernel,
        out_shape=jax.ShapeDtypeStruct((ROW, ROW), f32),
        in_specs=[vmem] * 5,
        out_specs=vmem,
        cost_estimate=pl.CostEstimate(flops=10_000_000, bytes_accessed=40_000_000, transcendentals=0),
        compiler_params=pltpu.CompilerParams(vmem_limit_bytes=4 << 20),
        name="pick",
    )(wanted, *tables)
    arrived = within_plane(picked.reshape(16, 8, ROW)).reshape(ROW, ROW)

    y, local = pl.pallas_call(
        perturb_kernel,
        out_shape=(jax.ShapeDtypeStruct(x.shape, x.dtype), jax.ShapeDtypeStruct((ROW, ROW), f32)),
        in_specs=[vmem, vmem, vmem, hbm],
        out_specs=(hbm, vmem),
        scratch_shapes=[
            pltpu.VMEM((4 * ROW, ROW), f32),
            pltpu.VMEM(x.shape, x.dtype),
            pltpu.VMEM(x.shape, x.dtype),
            pltpu.SemaphoreType.DMA((PARTS,)),
            pltpu.SemaphoreType.DMA((PARTS,)),
        ],
        cost_estimate=pl.CostEstimate(flops=10_000_000, bytes_accessed=9_000_000, transcendentals=0),
        compiler_params=pltpu.CompilerParams(vmem_limit_bytes=52 << 20),
        name="perturb",
    )(scalars, arrived, place, x)
    out = pl.pallas_call(
        integrals_kernel,
        out_shape=jax.ShapeDtypeStruct((2 * ROW, ROW), f32),
        in_specs=[vmem] * 5,
        out_specs=vmem,
        compiler_params=pltpu.CompilerParams(vmem_limit_bytes=4 << 20),
        name="integrals",
    )(local, sums, *others)
    perturbed = y.reshape(levels, ROW, 4, ROW).transpose(2, 0, 1, 3).reshape(tendencies.shape)
    integrals = out.reshape(ROW, 2, ROW).transpose(1, 0, 2).reshape(2, ROW * ROW)
    return perturbed, integrals


def solution(mesh):
    split = jax.sharding.Mesh(mesh.devices.reshape(4, 4, 4, 4), ("x", "z", "y", "lev"))
    band = ("x", "z", "y")
    in_specs = (P(band, None), P("lev"), P("lev"), P(band), P(None, "lev", band))
    out_specs = (P(None, "lev", band), P(None, band))
    return jax.shard_map(program, mesh=split, in_specs=in_specs, out_specs=out_specs, check_vma=False)
```

time: 50.7 us -> 49.1 us (0.968)
  local copies, waits for them, and re-layouts: 4.24 us -> 1.47 us
  Pallas kernels: 7.67 us -> 8.79 us
    unnamed x14 -> x10, local copies, waits for them, and re-layouts: 4.24 us -> 1.47 us
    pallas_call x4 -> x5, Pallas kernels: 7.67 us -> 8.79 us  [the longest x1 3.73 us: program(): pl.pallas_call(perturb_kernel, out_shape=(jax.ShapeDtypeStruct(x.shape, x...]
  transfers between devices with their start and end apart: 6 -> 6, of which waited for: 0 -> 0; matrix products, arithmetic and copies ran while one was open for 0% -> 0% of each run, Pallas kernels for 5% -> 17%
where the time goes in v2:
time: 49.1 us; the launch traced here: 48.8 us
  blocking collectives  25.4 us (52%)
  starting transfers between devices  12.4 us (25%)
  Pallas kernels  8.79 us (18%)
  local copies, waits for them, and re-layouts  1.47 us (3%)
  between operations  0.7 us (1%)
    all_to_all x2, blocking collectives, within_plane(): return lax.all_to_all(a, ('x', 'y'), 0, 0, tiled=True)  25.4 us
    ppermute x3, starting transfers between devices, along_z(): return lax.ppermute(a, 'z', [(i, (i + step) % 4) for i in range(4)])  10.5 us
    pallas_call x1, Pallas kernels, program(): pl.pallas_call(perturb_kernel, out_shape=(jax.ShapeDtypeStruct(x.shape, x...  3.73 us
    pallas_call x1, Pallas kernels, program(): pl.pallas_call(column_kernel, out_shape=(jax.ShapeDtypeStruct((2 * ROW +...  2.5 us
    ppermute x3, starting transfers between devices, across_lev(): return lax.ppermute(a, 'lev', [(i, i ^ flip) for i in range(4)])  1.94 us
    pallas_call x1, Pallas kernels, program(): pl.pallas_call(request_kernel, out_shape=(jax.ShapeDtypeStruct((ROW, ROW)...  1.6 us
    unnamed x10, local copies, waits for them, and re-layouts  1.47 us
  transfers between devices with their start and end apart: 6, of which 0 were waited for; matrix products, arithmetic and copies ran while one was open for 0% of the time, Pallas kernels for 17%

profile of v2, /device:TPU:32, one launch (start us, length us, event | category | flops | bytes accessed | tf_op | source)
XLA Modules:
  0.0 48.8 jit_solution(17091117297772643098)
XLA Ops:
  0.6 3.3 %collective-permute-start = (f32[128,128]{1,0:T(8,128)}, f32[128,128]{1,0:T(8,128)S(1)}, u32[]{:S(2)}, u32[]{:S(2)}) collective-permute-start(f32[128,128]{1,0:T(8,128)} %t0.1), channel_id=1, source_target_pairs={{0,16},{16,32},{32,48},{48,0},{1,17},{17,33},{33,49},{49,1},{2,18}... | collective-permute-start | bytes 196616 | tf_op jit(solution)/shard_map/ppermute | solution.py:16
  4.0 1.6 %request.1 = (s32[128,128]{1,0:T(8,128)}, s32[8,128]{1,0:T(8,128)}, f32[88,128]{1,0:T(8,128)}) custom-call(s32[1,128]{1,0:T(1,128)} %bitcast.30, f32[1,34]{1,0:T(1,128)} %bitcast.31, f32[1,34]{1,0:T(1,128)} %bitcast.32), custom_call_target="tpu_custom_call" | custom-call | tf_op jit(solution)/shard_map/request/pallas_call | solution.py:173
  5.6 0.0 copy-start
  5.6 0.8 %copy-done = f32[88,128]{1,0:T(8,128)S(1)} copy-done((f32[88,128]{1,0:T(8,128)S(1)}, f32[88,128]{1,0:T(8,128)}, u32[]{:S(2)}) %copy-start) | copy-done | bytes 45080
  6.4 0.0 copy-start.3
  6.4 0.7 %copy-done.3 = s32[8,128]{1,0:T(8,128)S(1)} copy-done((s32[8,128]{1,0:T(8,128)S(1)}, s32[8,128]{1,0:T(8,128)}, u32[]{:S(2)}) %copy-start.3) | copy-done | bytes 4120
  7.0 0.0 copy-start.2
  7.0 0.0 copy-start.4
  7.0 0.0 copy-start.1
  7.0 2.5 %columns.1 = (f32[264,128]{1,0:T(8,128)S(1)}, bf16[512,128]{1,0:T(8,128)(2,1)S(1)}) custom-call(f32[88,128]{1,0:T(8,128)S(1)} %copy-done, s32[8,128]{1,0:T(8,128)S(1)} %copy-done.3, bf16[34,512,128]{2,1,0:T(8,128)(2,1)} %bitcast.25), custom_call_target="tpu_custom_call" | custom-call | flops 10000000 | bytes 4500000 | tf_op jit(solution)/shard_map/columns/pallas_call | solution.py:187
  9.6 0.1 collective-permute-start.3
  9.7 0.2 collective-permute-start.4
  9.9 1.6 %collective-permute-start.5 = (f32[264,128]{1,0:T(8,128)S(1)}, f32[264,128]{1,0:T(8,128)S(1)}, u32[]{:S(2)}, u32[]{:S(2)}) collective-permute-start(f32[264,128]{1,0:T(8,128)S(1)} %get-tuple-element.15.s0), channel_id=1, source_target_pairs={{0,3},{1,2},{2,1},{3,0},{4,7},{5,6},{6,5},{7,4},{8,11},{9,10},{10,... | collective-permute-start | bytes 405512 | tf_op jit(solution)/shard_map/ppermute | solution.py:20
  11.5 0.0 copy-done.2
  11.5 4.5 %collective-permute-start.1 = (f32[128,128]{1,0:T(8,128)S(1)}, f32[128,128]{1,0:T(8,128)S(1)}, u32[]{:S(2)}, u32[]{:S(2)}) collective-permute-start(f32[128,128]{1,0:T(8,128)S(1)} %copy-done.2), channel_id=1, source_target_pairs={{0,32},{16,48},{32,0},{48,16},{1,33},{17,49},{33,1},{49,17},{2,34}... | collective-permute-start | bytes 196616 | tf_op jit(solution)/shard_map/ppermute | solution.py:16
  16.0 0.0 collective-permute-done.t1
  16.0 2.7 %collective-permute-start.2 = (f32[128,128]{1,0:T(8,128)S(1)}, f32[128,128]{1,0:T(8,128)S(1)}, u32[]{:S(2)}, u32[]{:S(2)}) collective-permute-start(f32[128,128]{1,0:T(8,128)S(1)} %copy-done.2), channel_id=1, source_target_pairs={{0,48},{16,0},{32,16},{48,32},{1,49},{17,1},{33,17},{49,33},{2,50}... | collective-permute-start | bytes 196616 | tf_op jit(solution)/shard_map/ppermute | solution.py:16
  18.7 0.0 copy-done.4
  18.7 14.5 %all_to_all.10 = s32[16,8,128]{2,1,0:T(8,128)S(1)} all-to-all(s32[16,8,128]{2,1,0:T(8,128)S(1)} %bitcast.28), channel_id=1, replica_groups=mesh['x'=4,'z'=4,'y'=4,'lev'=4] {'x','y'}, dimensions={0} | all-to-all | bytes 131072 | tf_op jit(solution)/shard_map/all_to_all | solution.py:24
  33.2 0.0 collective-permute-done.1.t2
  33.2 0.0 collective-permute-done.2.t3
  33.2 0.3 pick.1
  33.4 10.9 %all_to_all.11 = f32[16,8,128]{2,1,0:T(8,128)S(1)} all-to-all(f32[16,8,128]{2,1,0:T(8,128)S(1)} %bitcast.24), channel_id=1, replica_groups=mesh['x'=4,'z'=4,'y'=4,'lev'=4] {'x','y'}, dimensions={0} | all-to-all | bytes 131072 | tf_op jit(solution)/shard_map/all_to_all | solution.py:24
  44.3 0.0 copy-done.1
  44.3 3.7 %perturb.1 = (bf16[34,512,128]{2,1,0:T(8,128)(2,1)}, f32[128,128]{1,0:T(8,128)S(1)}) custom-call(f32[88,128]{1,0:T(8,128)S(1)} %copy-done.1, f32[128,128]{1,0:T(8,128)S(1)} %bitcast.22, bf16[512,128]{1,0:T(8,128)(2,1)S(1)} %get-tuple-element.12.place_ref, bf16[34,512,128]{2,1,0:T(8,128)(2,1)} %bitcast.26), custom_call_target="tpu_custom_call" | custom-call | flops 10000000 | bytes 9000000 | tf_op jit(solution)/shard_map/perturb/pallas_call | solution.py:214
  48.1 0.0 collective-permute-done.3.s1
  48.1 0.0 collective-permute-done.4.s2
  48.1 0.0 collective-permute-done.5.s3
  48.1 0.7 %integrals.1 = f32[256,128]{1,0:T(8,128)} custom-call(f32[128,128]{1,0:T(8,128)S(1)} %get-tuple-element.14.local_ref, f32[264,128]{1,0:T(8,128)S(1)} %get-tuple-element.15.s0, f32[264,128]{1,0:T(8,128)S(1)} %collective-permute-done.3.s1, f32[264,128]{1,0:T(8,128)S(1)} %collective-permute-done.4.s2, f32[264,128]{1,0:T(8,128)S(1)} %collective-permute-done.5.s3), custom_call_target="tpu_custom_call" | custom-call | tf_op jit(solution)/shard_map/integrals/pallas_call | solution.py:230
Async XLA Ops:
  0.6 15.4 %collective-permute-start = (f32[128,128]{1,0:T(8,128)}, f32[128,128]{1,0:T(8,128)S(1)}, u32[]{:S(2)}, u32[]{:S(2)}) collective-permute-start(f32[128,128]{1,0:T(8,128)} %t0.1), channel_id=1, source_target_pairs={{0,16},{16,32},{32,48},{48,0},{1,17},{17,33},{33,49},{49,1},{2,18}... | collective-permute-start | bytes 196616 | tf_op jit(solution)/shard_map/ppermute | solution.py:16
  5.6 0.8 %copy-start = (f32[88,128]{1,0:T(8,128)S(1)}, f32[88,128]{1,0:T(8,128)}, u32[]{:S(2)}) copy-start(f32[88,128]{1,0:T(8,128)} %get-tuple-element.9.scalars_ref) | copy-start | bytes 135172
  6.4 0.7 %copy-start.3 = (s32[8,128]{1,0:T(8,128)S(1)}, s32[8,128]{1,0:T(8,128)}, u32[]{:S(2)}) copy-start(s32[8,128]{1,0:T(8,128)} %get-tuple-element.11.pos_ref) | copy-start | bytes 12292
  7.0 4.5 %copy-start.2 = (f32[128,128]{1,0:T(8,128)S(1)}, f32[128,128]{1,0:T(8,128)}, u32[]{:S(2)}) copy-start(f32[128,128]{1,0:T(8,128)} %t0.1) | copy-start | bytes 196612
  7.0 11.6 %copy-start.4 = (s32[128,128]{1,0:T(8,128)S(1)}, s32[128,128]{1,0:T(8,128)}, u32[]{:S(2)}) copy-start(s32[128,128]{1,0:T(8,128)} %get-tuple-element.10) | copy-start | bytes 196612
  7.0 37.3 %copy-start.1 = (f32[88,128]{1,0:T(8,128)S(1)}, f32[88,128]{1,0:T(8,128)}, u32[]{:S(2)}) copy-start(f32[88,128]{1,0:T(8,128)} %get-tuple-element.9.scalars_ref) | copy-start | bytes 135172
  9.6 38.5 %collective-permute-start.3 = (f32[264,128]{1,0:T(8,128)S(1)}, f32[264,128]{1,0:T(8,128)S(1)}, u32[]{:S(2)}, u32[]{:S(2)}) collective-permute-start(f32[264,128]{1,0:T(8,128)S(1)} %get-tuple-element.15.s0), channel_id=1, source_target_pairs={{0,1},{1,0},{2,3},{3,2},{4,5},{5,4},{6,7},{7,6},{8,9},{9,8},{10,11... | collective-permute-start | bytes 405512 | tf_op jit(solution)/shard_map/ppermute | solution.py:20
  9.7 38.4 %collective-permute-start.4 = (f32[264,128]{1,0:T(8,128)S(1)}, f32[264,128]{1,0:T(8,128)S(1)}, u32[]{:S(2)}, u32[]{:S(2)}) collective-permute-start(f32[264,128]{1,0:T(8,128)S(1)} %get-tuple-element.15.s0), channel_id=1, source_target_pairs={{0,2},{1,3},{2,0},{3,1},{4,6},{5,7},{6,4},{7,5},{8,10},{9,11},{10,... | collective-permute-start | bytes 405512 | tf_op jit(solution)/shard_map/ppermute | solution.py:20
  9.9 38.2 %collective-permute-start.5 = (f32[264,128]{1,0:T(8,128)S(1)}, f32[264,128]{1,0:T(8,128)S(1)}, u32[]{:S(2)}, u32[]{:S(2)}) collective-permute-start(f32[264,128]{1,0:T(8,128)S(1)} %get-tuple-element.15.s0), channel_id=1, source_target_pairs={{0,3},{1,2},{2,1},{3,0},{4,7},{5,6},{6,5},{7,4},{8,11},{9,10},{10,... | collective-permute-start | bytes 405512 | tf_op jit(solution)/shard_map/ppermute | solution.py:20
  11.5 21.7 %collective-permute-start.1 = (f32[128,128]{1,0:T(8,128)S(1)}, f32[128,128]{1,0:T(8,128)S(1)}, u32[]{:S(2)}, u32[]{:S(2)}) collective-permute-start(f32[128,128]{1,0:T(8,128)S(1)} %copy-done.2), channel_id=1, source_target_pairs={{0,32},{16,48},{32,0},{48,16},{1,33},{17,49},{33,1},{49,17},{2,34}... | collective-permute-start | bytes 196616 | tf_op jit(solution)/shard_map/ppermute | solution.py:16
  16.0 17.2 %collective-permute-start.2 = (f32[128,128]{1,0:T(8,128)S(1)}, f32[128,128]{1,0:T(8,128)S(1)}, u32[]{:S(2)}, u32[]{:S(2)}) collective-permute-start(f32[128,128]{1,0:T(8,128)S(1)} %copy-done.2), channel_id=1, source_target_pairs={{0,48},{16,0},{32,16},{48,32},{1,49},{17,1},{33,17},{49,33},{2,50}... | collective-permute-start | bytes 196616 | tf_op jit(solution)/shard_map/ppermute | solution.py:16

commit v3 on v2

--- a/solution.py
+++ b/solution.py
@@ -6,22 +6,24 @@
 from jax.sharding import PartitionSpec as P
 
 
+OFFSET = (0, 3, 1, 2)
+SOURCE = (0, 2, 1, 3)
 ROW = 128
 LEVELS = 40
 PARTS = 8
 PART = 4 * ROW // PARTS
 
 
-def along_z(a, step):
-    return lax.ppermute(a, "z", [(i, (i + step) % 4) for i in range(4)])
+def along_z(a):
+    pairs = []
+    for z in range(4):
+        for lev in range(4):
+            pairs.append((((z + OFFSET[lev]) % 4) * 4 + SOURCE[lev], z * 4 + lev))
+    return lax.ppermute(a, ("z", "lev"), pairs)
 
 
 def across_lev(a, flip):
     return lax.ppermute(a, "lev", [(i, i ^ flip) for i in range(4)])
-
-
-def within_plane(a):
-    return lax.all_to_all(a, ("x", "y"), 0, 0, tiled=True)
 
 
 def iota(shape, dim):
@@ -48,25 +50,21 @@
     return high, mid, low
 
 
-def request_kernel(source_ref, taper_ref, thick_ref, ids_ref, pos_ref, scalars_ref):
+def request_kernel(source_ref, taper_ref, thick_ref, ids_ref, scalars_ref):
     source = source_ref[...]
     band, row = source >> 7, source & 127
-    group = (band >> 4) * 4 + (band & 3)
-    my_z = lax.axis_index("z")
-    table = (my_z - ((band >> 2) & 3)) & 3
-    member = iota((16, ROW), 0) == group
+    offset = ((band >> 2) - lax.axis_index("z")) & 3
+    lev = jnp.where(offset == 3, 1, jnp.where(offset == 0, 0, offset + 1))
+    holder = ((band >> 4) * 4 + (band & 3)) * 4 + lev
+    member = iota((64, ROW), 0) == holder
     before = onehot(iota((ROW, ROW), 0) < iota((ROW, ROW), 1))
     count = dot(onehot(member), before)
     rank = jnp.sum(jnp.where(member, count, 0.0), axis=0, keepdims=True)
-    pos = group * 8 + rank.astype(jnp.int32)
-    slot = onehot(iota((ROW, ROW), 0) == pos)
-
-    def everywhere(v):
-        return jnp.broadcast_to(v.astype(jnp.float32), (ROW, ROW)).astype(jnp.bfloat16)
-
-    ids = dot_nt(slot, everywhere(table)) * 128.0 + dot_nt(slot, everywhere(row))
-    ids_ref[...] = ids.astype(jnp.int32)
-    pos_ref[...] = jnp.broadcast_to(pos, pos_ref.shape)
+    pos = holder * 2 + rank.astype(jnp.int32)
+    slot = iota((ROW, ROW), 0)
+    asked = (slot >> 3) * 8 + lax.axis_index("lev") * 2 + (slot & 1)
+    rows = jnp.broadcast_to(row.astype(jnp.float32), (ROW, ROW)).astype(jnp.bfloat16)
+    ids_ref[...] = dot_nt(onehot(asked == pos), rows).astype(jnp.int32)
 
     taper, thick = taper_ref[...], thick_ref[...]
     levels = taper.shape[1]
@@ -78,19 +76,14 @@
 
     scalars_ref[0:LEVELS, :] = one_per_row(taper)
     scalars_ref[LEVELS : 2 * LEVELS, :] = one_per_row(taper * thick)
-    scalars_ref[2 * LEVELS :, :] = jnp.broadcast_to(jnp.sum(thick * thick, axis=1, keepdims=True), (8, ROW))
-
-
-def pick_kernel(ids_ref, t0, t1, t2, t3, out_ref):
-    ids = ids_ref[...]
-    lane = iota((ROW, ROW), 1)
-    total = None
-    for c, ref in enumerate((t0, t1, t2, t3)):
-        pick = onehot(ids == lane + c * ROW)
-        high, mid, low = three_parts(ref[...])
-        part = (dot(pick, high), dot(pick, mid), dot(pick, low))
-        total = part if total is None else tuple(a + b for a, b in zip(total, part))
-    out_ref[...] = (total[0] + total[1]) + total[2]
+    scalars_ref[2 * LEVELS : 2 * LEVELS + 8, :] = jnp.broadcast_to(jnp.sum(thick * thick, axis=1, keepdims=True), (8, ROW))
+    scalars_ref[2 * LEVELS + 8 :, :] = jnp.broadcast_to(pos.astype(jnp.float32), (8, ROW))
+
+
+def pick_kernel(ids_ref, table_ref, out_ref):
+    pick = onehot(ids_ref[...] == iota((ROW, ROW), 1))
+    high, mid, low = three_parts(table_ref[...])
+    out_ref[...] = (dot(pick, high) + dot(pick, mid)) + dot(pick, low)
 
 
 def fetches(x_hbm, x_ref, sems):
@@ -103,10 +96,10 @@
     return fetch
 
 
-def column_kernel(scalars_ref, pos_ref, x_hbm, sums_ref, place_ref, acc_ref, x_ref, sems):
+def column_kernel(scalars_ref, x_hbm, sums_ref, place_ref, acc_ref, x_ref, sems):
     levels = x_ref.shape[0]
     fetch = fetches(x_hbm, x_ref, sems)
-    pos = jnp.broadcast_to(pos_ref[0:1, :].astype(jnp.float32), (ROW, ROW)).astype(jnp.bfloat16)
+    pos = jnp.broadcast_to(scalars_ref[2 * LEVELS + 8 : 2 * LEVELS + 9, :], (ROW, ROW)).astype(jnp.bfloat16)
     expand = onehot(iota((4 * ROW, ROW), 0) >> 2 == iota((4 * ROW, ROW), 1))
     slot = dot_nt(expand, pos).astype(jnp.int32)
     place_ref[...] = onehot(slot == iota((4 * ROW, ROW), 1))
@@ -124,7 +117,7 @@
     lax.fori_loop(0, PARTS, chunk, 0)
     for k in range(2):
         sums_ref[pl.ds(k * ROW, ROW), :] = acc_ref[pl.ds(2 + k, ROW, stride=4), :]
-    sums_ref[pl.ds(2 * ROW, 8), :] = scalars_ref[2 * LEVELS :, :]
+    sums_ref[pl.ds(2 * ROW, 8), :] = scalars_ref[2 * LEVELS : 2 * LEVELS + 8, :]
 
 
 def perturb_kernel(scalars_ref, arrived_ref, place_ref, x_hbm, y_hbm, clipped_ref, local_ref, x_ref, y_ref, in_sems, sems):
@@ -133,7 +126,6 @@
     parts = three_parts(jnp.tanh(arrived_ref[...]))
     place = place_ref[...]
     local_ref[...] = (dot(place, parts[0]) + dot(place, parts[1])) + dot(place, parts[2])
-    clipped_ref[...] = local_ref[pl.ds(0, ROW, stride=4), :]
 
     def store(i):
         rows = pl.ds(pl.multiple_of(i * PART, PART), PART)
@@ -151,6 +143,8 @@
         return carry
 
     lax.fori_loop(0, PARTS, chunk, 0)
+
+    clipped_ref[...] = local_ref[pl.ds(0, ROW, stride=4), :]
     for i in range(PARTS):
         store(i).wait()
 
@@ -168,26 +162,21 @@
     levels = tendencies.shape[1]
     f32, s32 = jnp.float32, jnp.int32
 
-    tables = [pattern] + [along_z(pattern, k) for k in (1, 2, 3)]
-    scalar_rows = 2 * LEVELS + 8
-    ids, pos, scalars = pl.pallas_call(
+    table = along_z(pattern)
+    ids, scalars = pl.pallas_call(
         request_kernel,
-        out_shape=(
-            jax.ShapeDtypeStruct((ROW, ROW), s32),
-            jax.ShapeDtypeStruct((8, ROW), s32),
-            jax.ShapeDtypeStruct((scalar_rows, ROW), f32),
-        ),
+        out_shape=(jax.ShapeDtypeStruct((ROW, ROW), s32), jax.ShapeDtypeStruct((2 * LEVELS + 16, ROW), f32)),
         in_specs=[vmem, vmem, vmem],
-        out_specs=(vmem, vmem, vmem),
+        out_specs=(vmem, vmem),
         name="request",
     )(block_source.reshape(1, ROW), taper.reshape(1, levels), thickness.reshape(1, levels))
-    wanted = within_plane(ids.reshape(16, 8, ROW)).reshape(ROW, ROW)
+    wanted = lax.all_to_all(ids.reshape(16, 8, ROW), ("x", "y"), 0, 0, tiled=True).reshape(ROW, ROW)
 
     x = tendencies.reshape(4, levels, ROW, ROW).transpose(1, 2, 0, 3).reshape(levels, 4 * ROW, ROW)
     sums, place = pl.pallas_call(
         column_kernel,
         out_shape=(jax.ShapeDtypeStruct((2 * ROW + 8, ROW), f32), jax.ShapeDtypeStruct((4 * ROW, ROW), jnp.bfloat16)),
-        in_specs=[vmem, vmem, hbm],
+        in_specs=[vmem, hbm],
         out_specs=(vmem, vmem),
         scratch_shapes=[
             pltpu.VMEM((4 * ROW, ROW), f32),
@@ -197,19 +186,18 @@
         cost_estimate=pl.CostEstimate(flops=10_000_000, bytes_accessed=4_500_000, transcendentals=0),
         compiler_params=pltpu.CompilerParams(vmem_limit_bytes=52 << 20),
         name="columns",
-    )(scalars, pos, x)
+    )(scalars, x)
     others = [across_lev(sums, flip) for flip in (1, 2, 3)]
 
     picked = pl.pallas_call(
         pick_kernel,
         out_shape=jax.ShapeDtypeStruct((ROW, ROW), f32),
-        in_specs=[vmem] * 5,
+        in_specs=[vmem] * 2,
         out_specs=vmem,
-        cost_estimate=pl.CostEstimate(flops=10_000_000, bytes_accessed=40_000_000, transcendentals=0),
         compiler_params=pltpu.CompilerParams(vmem_limit_bytes=4 << 20),
         name="pick",
-    )(wanted, *tables)
-    arrived = within_plane(picked.reshape(16, 8, ROW)).reshape(ROW, ROW)
+    )(wanted, table)
+    arrived = lax.all_to_all(picked.reshape(64, 2, ROW), ("x", "y", "lev"), 0, 0, tiled=True).reshape(ROW, ROW)
 
     y, local = pl.pallas_call(
         perturb_kernel,

time: 49.1 us -> 45.2 us (0.921)
  the two profiles are of different devices: /device:TPU:32 before, /device:TPU:1 now
where the time goes in v3:
time: 45.2 us; the launch traced here: 44.8 us
  starting transfers between devices  18 us (40%)
  blocking collectives  15.7 us (35%)
  Pallas kernels  8.67 us (19%)
  waiting for transfers between devices  1.03 us (2%)
  local copies, waits for them, and re-layouts  0.8 us (2%)
  between operations  0.71 us (2%)
    all_to_all x1, blocking collectives, program(): lax.all_to_all(picked.reshape(64, 2, ROW), ('x', 'y', 'lev'), 0, 0, tiled...  15.7 us
    ppermute x1, starting transfers between devices, along_z(): return lax.ppermute(a, ('z', 'lev'), pairs)  8.86 us
    all_to_all x1, starting transfers between devices, program(): lax.all_to_all(ids.reshape(16, 8, ROW), ('x', 'y'), 0, 0, tiled=True)  6.89 us
    pallas_call x1, Pallas kernels, program(): pl.pallas_call(perturb_kernel, out_shape=(jax.ShapeDtypeStruct(x.shape, x...  3.73 us
    pallas_call x1, Pallas kernels, program(): pl.pallas_call(column_kernel, out_shape=(jax.ShapeDtypeStruct((2 * ROW +...  2.46 us
    ppermute x3, starting transfers between devices, across_lev(): return lax.ppermute(a, 'lev', [(i, i ^ flip) for i in range(4)])  2.22 us
    pallas_call x1, Pallas kernels, program(): pl.pallas_call(request_kernel, out_shape=(jax.ShapeDtypeStruct((ROW, ROW)...  1.61 us
    all_to_all x1, waiting for transfers between devices, program(): lax.all_to_all(ids.reshape(16, 8, ROW), ('x', 'y'), 0, 0, tiled=True)  1.02 us
  transfers between devices with their start and end apart: 5, of which 1 were waited for; matrix products, arithmetic and copies ran while one was open for 0% of the time, Pallas kernels for 18%

profile of v3, /device:TPU:1, one launch (start us, length us, event | category | flops | bytes accessed | tf_op | source)
XLA Modules:
  0.0 44.8 jit_solution(2739740420730259863)
XLA Ops:
  0.6 8.9 %collective-permute-start = (f32[128,128]{1,0:T(8,128)}, f32[128,128]{1,0:T(8,128)S(1)}, u32[]{:S(2)}, u32[]{:S(2)}) collective-permute-start(f32[128,128]{1,0:T(8,128)} %param.5), channel_id=1, source_target_pairs={{0,0},{50,1},{17,2},{35,3},{16,16},{2,17},{33,18},{51,19},{32,32},... | collective-permute-start | bytes 196616 | tf_op jit(solution)/shard_map/ppermute | solution.py:22
  9.5 1.6 %request.1 = (s32[128,128]{1,0:T(8,128)}, f32[96,128]{1,0:T(8,128)}) custom-call(s32[1,128]{1,0:T(1,128)} %bitcast.30, f32[1,34]{1,0:T(1,128)} %bitcast.31, f32[1,34]{1,0:T(1,128)} %bitcast.32), custom_call_target="tpu_custom_call" | custom-call | tf_op jit(solution)/shard_map/request/pallas_call | solution.py:166
  11.1 0.0 copy-start.1
  11.1 6.9 %all-to-all-start = ((s32[16,8,128]{2,1,0:T(8,128)}), s32[16,8,128]{2,1,0:T(8,128)S(1)}, u32[]{:S(2)}, u32[]{:S(2)}) async-start(s32[16,8,128]{2,1,0:T(8,128)} %bitcast.28), calls=%async_computation | async-start | bytes 131072 | tf_op jit(solution)/shard_map/all_to_all | solution.py:173
  18.0 0.0 copy-start
  18.0 0.8 %copy-done = f32[96,128]{1,0:T(8,128)S(1)} copy-done((f32[96,128]{1,0:T(8,128)S(1)}, f32[96,128]{1,0:T(8,128)}, u32[]{:S(2)}) %copy-start) | copy-done | bytes 49176
  18.8 2.5 %columns.1 = (f32[264,128]{1,0:T(8,128)S(1)}, bf16[512,128]{1,0:T(8,128)(2,1)S(1)}) custom-call(f32[96,128]{1,0:T(8,128)S(1)} %copy-done, bf16[34,512,128]{2,1,0:T(8,128)(2,1)} %bitcast.25), custom_call_target="tpu_custom_call" | custom-call | flops 10000000 | bytes 4500000 | tf_op jit(solution)/shard_map/columns/pallas_call | solution.py:176
  21.3 0.1 collective-permute-start.1
  21.4 1.6 %collective-permute-start.2 = (f32[264,128]{1,0:T(8,128)S(1)}, f32[264,128]{1,0:T(8,128)S(1)}, u32[]{:S(2)}, u32[]{:S(2)}) collective-permute-start(f32[264,128]{1,0:T(8,128)S(1)} %get-tuple-element.13.s0), channel_id=1, source_target_pairs={{0,2},{1,3},{2,0},{3,1},{4,6},{5,7},{6,4},{7,5},{8,10},{9,11},{10,... | collective-permute-start | bytes 405512 | tf_op jit(solution)/shard_map/ppermute | solution.py:26
  23.0 0.5 %collective-permute-start.3 = (f32[264,128]{1,0:T(8,128)S(1)}, f32[264,128]{1,0:T(8,128)S(1)}, u32[]{:S(2)}, u32[]{:S(2)}) collective-permute-start(f32[264,128]{1,0:T(8,128)S(1)} %get-tuple-element.13.s0), channel_id=1, source_target_pairs={{0,3},{1,2},{2,1},{3,0},{4,7},{5,6},{6,5},{7,4},{8,11},{9,10},{10,... | collective-permute-start | bytes 405512 | tf_op jit(solution)/shard_map/ppermute | solution.py:26
  23.5 1.0 %all-to-all-done = s32[16,8,128]{2,1,0:T(8,128)S(1)} async-done(((s32[16,8,128]{2,1,0:T(8,128)}), s32[16,8,128]{2,1,0:T(8,128)S(1)}, u32[]{:S(2)}, u32[]{:S(2)}) %all-to-all-start) | async-done | bytes 65568 | tf_op jit(solution)/shard_map/all_to_all | solution.py:173
  24.5 0.0 collective-permute-done.table_ref
  24.5 0.2 pick.1
  24.7 15.7 %all_to_all.10 = f32[64,2,128]{2,1,0:T(2,128)S(1)} all-to-all(f32[64,2,128]{2,1,0:T(2,128)S(1)} %bitcast.24), channel_id=1, replica_groups=mesh['x'=4,'z'=4,'y'=4,'lev'=4] {'x','y','lev'}, dimensions={0} | all-to-all | bytes 131072 | tf_op jit(solution)/shard_map/all_to_all | solution.py:200
  40.4 0.0 copy-done.1
  40.4 3.7 %perturb.1 = (bf16[34,512,128]{2,1,0:T(8,128)(2,1)}, f32[128,128]{1,0:T(8,128)S(1)}) custom-call(f32[96,128]{1,0:T(8,128)S(1)} %copy-done.1, f32[128,128]{1,0:T(8,128)S(1)} %bitcast.22, bf16[512,128]{1,0:T(8,128)(2,1)S(1)} %get-tuple-element.10.place_ref, bf16[34,512,128]{2,1,0:T(8,128)(2,1)} %bitcast.26), custom_call_target="tpu_custom_call" | custom-call | flops 10000000 | bytes 9000000 | tf_op jit(solution)/shard_map/perturb/pallas_call | solution.py:202
  44.1 0.0 collective-permute-done.1.s1
  44.1 0.0 collective-permute-done.2.s2
  44.1 0.0 collective-permute-done.3.s3
  44.1 0.7 %integrals.1 = f32[256,128]{1,0:T(8,128)} custom-call(f32[128,128]{1,0:T(8,128)S(1)} %get-tuple-element.12.local_ref, f32[264,128]{1,0:T(8,128)S(1)} %get-tuple-element.13.s0, f32[264,128]{1,0:T(8,128)S(1)} %collective-permute-done.1.s1, f32[264,128]{1,0:T(8,128)S(1)} %collective-permute-done.2.s2, f32[264,128]{1,0:T(8,128)S(1)} %collective-permute-done.3.s3), custom_call_target="tpu_custom_call" | custom-call | tf_op jit(solution)/shard_map/integrals/pallas_call | solution.py:218
Async XLA Ops:
  0.6 23.9 %collective-permute-start = (f32[128,128]{1,0:T(8,128)}, f32[128,128]{1,0:T(8,128)S(1)}, u32[]{:S(2)}, u32[]{:S(2)}) collective-permute-start(f32[128,128]{1,0:T(8,128)} %param.5), channel_id=1, source_target_pairs={{0,0},{50,1},{17,2},{35,3},{16,16},{2,17},{33,18},{51,19},{32,32},... | collective-permute-start | bytes 196616 | tf_op jit(solution)/shard_map/ppermute | solution.py:22
  11.1 29.3 %copy-start.1 = (f32[96,128]{1,0:T(8,128)S(1)}, f32[96,128]{1,0:T(8,128)}, u32[]{:S(2)}) copy-start(f32[96,128]{1,0:T(8,128)} %get-tuple-element.8.scalars_ref) | copy-start | bytes 147460
  11.1 13.4 %all-to-all-start = ((s32[16,8,128]{2,1,0:T(8,128)}), s32[16,8,128]{2,1,0:T(8,128)S(1)}, u32[]{:S(2)}, u32[]{:S(2)}) async-start(s32[16,8,128]{2,1,0:T(8,128)} %bitcast.28), calls=%async_computation | async-start | bytes 131072 | tf_op jit(solution)/shard_map/all_to_all | solution.py:173
  18.0 0.8 %copy-start = (f32[96,128]{1,0:T(8,128)S(1)}, f32[96,128]{1,0:T(8,128)}, u32[]{:S(2)}) copy-start(f32[96,128]{1,0:T(8,128)} %get-tuple-element.8.scalars_ref) | copy-start | bytes 147460
  21.3 22.8 %collective-permute-start.1 = (f32[264,128]{1,0:T(8,128)S(1)}, f32[264,128]{1,0:T(8,128)S(1)}, u32[]{:S(2)}, u32[]{:S(2)}) collective-permute-start(f32[264,128]{1,0:T(8,128)S(1)} %get-tuple-element.13.s0), channel_id=1, source_target_pairs={{0,1},{1,0},{2,3},{3,2},{4,5},{5,4},{6,7},{7,6},{8,9},{9,8},{10,11... | collective-permute-start | bytes 405512 | tf_op jit(solution)/shard_map/ppermute | solution.py:26
  21.4 22.8 %collective-permute-start.2 = (f32[264,128]{1,0:T(8,128)S(1)}, f32[264,128]{1,0:T(8,128)S(1)}, u32[]{:S(2)}, u32[]{:S(2)}) collective-permute-start(f32[264,128]{1,0:T(8,128)S(1)} %get-tuple-element.13.s0), channel_id=1, source_target_pairs={{0,2},{1,3},{2,0},{3,1},{4,6},{5,7},{6,4},{7,5},{8,10},{9,11},{10,... | collective-permute-start | bytes 405512 | tf_op jit(solution)/shard_map/ppermute | solution.py:26
  23.0 21.2 %collective-permute-start.3 = (f32[264,128]{1,0:T(8,128)S(1)}, f32[264,128]{1,0:T(8,128)S(1)}, u32[]{:S(2)}, u32[]{:S(2)}) collective-permute-start(f32[264,128]{1,0:T(8,128)S(1)} %get-tuple-element.13.s0), channel_id=1, source_target_pairs={{0,3},{1,2},{2,1},{3,0},{4,7},{5,6},{6,5},{7,4},{8,11},{9,10},{10,... | collective-permute-start | bytes 405512 | tf_op jit(solution)/shard_map/ppermute | solution.py:26

commit v4 on v3

--- a/solution.py
+++ b/solution.py
@@ -22,6 +22,10 @@
     return lax.ppermute(a, ("z", "lev"), pairs)
 
 
+def along_y(a, step):
+    return lax.ppermute(a, "y", [(y, (y + step) % 4) for y in range(4)])
+
+
 def across_lev(a, flip):
     return lax.ppermute(a, "lev", [(i, i ^ flip) for i in range(4)])
 
@@ -55,16 +59,21 @@
     band, row = source >> 7, source & 127
     offset = ((band >> 2) - lax.axis_index("z")) & 3
     lev = jnp.where(offset == 3, 1, jnp.where(offset == 0, 0, offset + 1))
-    holder = ((band >> 4) * 4 + (band & 3)) * 4 + lev
+    table = (lax.axis_index("y") - band) & 3
+    holder = ((band >> 4) * 4 + lev) * 4 + table
     member = iota((64, ROW), 0) == holder
     before = onehot(iota((ROW, ROW), 0) < iota((ROW, ROW), 1))
     count = dot(onehot(member), before)
     rank = jnp.sum(jnp.where(member, count, 0.0), axis=0, keepdims=True)
     pos = holder * 2 + rank.astype(jnp.int32)
     slot = iota((ROW, ROW), 0)
-    asked = (slot >> 3) * 8 + lax.axis_index("lev") * 2 + (slot & 1)
-    rows = jnp.broadcast_to(row.astype(jnp.float32), (ROW, ROW)).astype(jnp.bfloat16)
-    ids_ref[...] = dot_nt(onehot(asked == pos), rows).astype(jnp.int32)
+    asked = onehot(((slot >> 5) * 4 + lax.axis_index("lev")) * 8 + (slot & 7) == pos)
+
+    def everywhere(v):
+        return jnp.broadcast_to(v.astype(jnp.float32), (ROW, ROW)).astype(jnp.bfloat16)
+
+    ids = dot_nt(asked, everywhere(table)) * 128.0 + dot_nt(asked, everywhere(row))
+    ids_ref[...] = ids.astype(jnp.int32)
 
     taper, thick = taper_ref[...], thick_ref[...]
     levels = taper.shape[1]
@@ -80,10 +89,14 @@
     scalars_ref[2 * LEVELS + 8 :, :] = jnp.broadcast_to(pos.astype(jnp.float32), (8, ROW))
 
 
-def pick_kernel(ids_ref, table_ref, out_ref):
-    pick = onehot(ids_ref[...] == iota((ROW, ROW), 1))
-    high, mid, low = three_parts(table_ref[...])
-    out_ref[...] = (dot(pick, high) + dot(pick, mid)) + dot(pick, low)
+def pick_kernel(ids_ref, t0, t1, t2, t3, out_ref):
+    ids, lane = ids_ref[...], iota((ROW, ROW), 1)
+    total = None
+    for c, ref in enumerate((t0, t1, t2, t3)):
+        pick = onehot(ids == lane + c * ROW)
+        part = tuple(dot(pick, v) for v in three_parts(ref[...]))
+        total = part if total is None else tuple(a + b for a, b in zip(total, part))
+    out_ref[...] = (total[0] + total[1]) + total[2]
 
 
 def fetches(x_hbm, x_ref, sems):
@@ -170,7 +183,8 @@
         out_specs=(vmem, vmem),
         name="request",
     )(block_source.reshape(1, ROW), taper.reshape(1, levels), thickness.reshape(1, levels))
-    wanted = lax.all_to_all(ids.reshape(16, 8, ROW), ("x", "y"), 0, 0, tiled=True).reshape(ROW, ROW)
+    wanted = lax.all_to_all(ids.reshape(4, 32, ROW), "x", 0, 0, tiled=True).reshape(ROW, ROW)
+    tables = [table] + [along_y(table, k) for k in (1, 2, 3)]
 
     x = tendencies.reshape(4, levels, ROW, ROW).transpose(1, 2, 0, 3).reshape(levels, 4 * ROW, ROW)
     sums, place = pl.pallas_call(
@@ -192,12 +206,12 @@
     picked = pl.pallas_call(
         pick_kernel,
         out_shape=jax.ShapeDtypeStruct((ROW, ROW), f32),
-        in_specs=[vmem] * 2,
+        in_specs=[vmem] * 5,
         out_specs=vmem,
         compiler_params=pltpu.CompilerParams(vmem_limit_bytes=4 << 20),
         name="pick",
-    )(wanted, table)
-    arrived = lax.all_to_all(picked.reshape(64, 2, ROW), ("x", "y", "lev"), 0, 0, tiled=True).reshape(ROW, ROW)
+    )(wanted, *tables)
+    arrived = lax.all_to_all(picked.reshape(16, 8, ROW), ("x", "lev"), 0, 0, tiled=True).reshape(ROW, ROW)
 
     y, local = pl.pallas_call(
         perturb_kernel,

time: 45.2 us -> 44.3 us (0.980)
  blocking collectives: 15.7 us -> 11.3 us
  starting transfers between devices: 18 us -> 20.2 us
  waiting for transfers between devices: 1.03 us -> 2.16 us
    ppermute x0 -> x3, starting transfers between devices: none -> 4.99 us  [along_y(): return lax.ppermute(a, 'y', [(y, (y + step) % 4) for y in range(4)])]
    all_to_all x1, blocking collectives: 15.7 us -> 11.3 us  [program(): lax.all_to_all(picked.reshape(16, 8, ROW), ('x', 'lev'), 0, 0, tiled=True)]
    all_to_all x1, starting transfers between devices: 6.89 us -> 4.15 us  [program(): lax.all_to_all(ids.reshape(4, 32, ROW), 'x', 0, 0, tiled=True)]
    ppermute x1, waiting for transfers between devices: 0.01 us -> 2.15 us  [along_z(): return lax.ppermute(a, ('z', 'lev'), pairs)]
    all_to_all x1, waiting for transfers between devices: 1.02 us -> 0.01 us  [program(): lax.all_to_all(ids.reshape(4, 32, ROW), 'x', 0, 0, tiled=True)]
  transfers between devices with their start and end apart: 5 -> 8, of which waited for: 1 -> 1; matrix products, arithmetic and copies ran while one was open for 0% -> 0% of each run, Pallas kernels for 18% -> 18%
where the time goes in v4:
time: 44.3 us; the launch traced here: 44 us
  starting transfers between devices  20.2 us (46%)
  blocking collectives  11.3 us (26%)
  Pallas kernels  8.75 us (20%)
  waiting for transfers between devices  2.16 us (5%)
  local copies, waits for them, and re-layouts  0.8 us (2%)
  between operations  0.7 us (2%)
    all_to_all x1, blocking collectives, program(): lax.all_to_all(picked.reshape(16, 8, ROW), ('x', 'lev'), 0, 0, tiled=True)  11.3 us
    ppermute x1, starting transfers between devices, along_z(): return lax.ppermute(a, ('z', 'lev'), pairs)  8.86 us
    ppermute x3, starting transfers between devices, along_y(): return lax.ppermute(a, 'y', [(y, (y + step) % 4) for y in range(4)])  4.99 us
    all_to_all x1, starting transfers between devices, program(): lax.all_to_all(ids.reshape(4, 32, ROW), 'x', 0, 0, tiled=True)  4.15 us
    pallas_call x1, Pallas kernels, program(): pl.pallas_call(perturb_kernel, out_shape=(jax.ShapeDtypeStruct(x.shape, x...  3.73 us
    pallas_call x1, Pallas kernels, program(): pl.pallas_call(column_kernel, out_shape=(jax.ShapeDtypeStruct((2 * ROW +...  2.45 us
    ppermute x3, starting transfers between devices, across_lev(): return lax.ppermute(a, 'lev', [(i, i ^ flip) for i in range(4)])  2.22 us
    ppermute x1, waiting for transfers between devices, along_z(): return lax.ppermute(a, ('z', 'lev'), pairs)  2.15 us
  transfers between devices with their start and end apart: 8, of which 1 were waited for; matrix products, arithmetic and copies ran while one was open for 0% of the time, Pallas kernels for 18%

profile of v4, /device:TPU:1, one launch (start us, length us, event | category | flops | bytes accessed | tf_op | source)
XLA Modules:
  0.0 44.0 jit_solution(600673023642935893)
XLA Ops:
  0.6 8.9 %collective-permute-start = (f32[128,128]{1,0:T(8,128)}, f32[128,128]{1,0:T(8,128)S(1)}, u32[]{:S(2)}, u32[]{:S(2)}) collective-permute-start(f32[128,128]{1,0:T(8,128)} %param.5), channel_id=1, source_target_pairs={{0,0},{50,1},{17,2},{35,3},{16,16},{2,17},{33,18},{51,19},{32,32},... | collective-permute-start | bytes 196616 | tf_op jit(solution)/shard_map/ppermute | solution.py:22
  9.5 2.1 %collective-permute-done.t0 = f32[128,128]{1,0:T(8,128)S(1)} collective-permute-done((f32[128,128]{1,0:T(8,128)}, f32[128,128]{1,0:T(8,128)S(1)}, u32[]{:S(2)}, u32[]{:S(2)}) %collective-permute-start) | collective-permute-done | bytes 65568 | tf_op jit(solution)/shard_map/ppermute | solution.py:22
  11.6 1.3 %collective-permute-start.1 = (f32[128,128]{1,0:T(8,128)S(1)}, f32[128,128]{1,0:T(8,128)S(1)}, u32[]{:S(2)}, u32[]{:S(2)}) collective-permute-start(f32[128,128]{1,0:T(8,128)S(1)} %collective-permute-done.t0), channel_id=1, source_target_pairs={{0,4},{4,8},{8,12},{12,0},{1,5},{5,9},{9,13},{13,1},{2,6},{6,10},{... | collective-permute-start | bytes 196616 | tf_op jit(solution)/shard_map/ppermute | solution.py:26
  12.9 2.6 %collective-permute-start.2 = (f32[128,128]{1,0:T(8,128)S(1)}, f32[128,128]{1,0:T(8,128)S(1)}, u32[]{:S(2)}, u32[]{:S(2)}) collective-permute-start(f32[128,128]{1,0:T(8,128)S(1)} %collective-permute-done.t0), channel_id=1, source_target_pairs={{0,8},{4,12},{8,0},{12,4},{1,9},{5,13},{9,1},{13,5},{2,10},{6,14},... | collective-permute-start | bytes 196616 | tf_op jit(solution)/shard_map/ppermute | solution.py:26
  15.6 1.1 %collective-permute-start.3 = (f32[128,128]{1,0:T(8,128)S(1)}, f32[128,128]{1,0:T(8,128)S(1)}, u32[]{:S(2)}, u32[]{:S(2)}) collective-permute-start(f32[128,128]{1,0:T(8,128)S(1)} %collective-permute-done.t0), channel_id=1, source_target_pairs={{0,12},{4,0},{8,4},{12,8},{1,13},{5,1},{9,5},{13,9},{2,14},{6,2},{... | collective-permute-start | bytes 196616 | tf_op jit(solution)/shard_map/ppermute | solution.py:26
  16.6 1.6 %request.1 = (s32[128,128]{1,0:T(8,128)}, f32[96,128]{1,0:T(8,128)}) custom-call(s32[1,128]{1,0:T(1,128)} %bitcast.30, f32[1,34]{1,0:T(1,128)} %bitcast.31, f32[1,34]{1,0:T(1,128)} %bitcast.32), custom_call_target="tpu_custom_call" | custom-call | tf_op jit(solution)/shard_map/request/pallas_call | solution.py:179
  18.2 0.0 copy-start.1
  18.2 4.1 %all-to-all-start = ((s32[4,32,128]{2,1,0:T(8,128)}), s32[4,32,128]{2,1,0:T(8,128)S(1)}, u32[]{:S(2)}, u32[]{:S(2)}) async-start(s32[4,32,128]{2,1,0:T(8,128)} %bitcast.28), calls=%async_computation | async-start | bytes 131072 | tf_op jit(solution)/shard_map/all_to_all | solution.py:186
  22.4 0.0 copy-start
  22.4 0.8 %copy-done = f32[96,128]{1,0:T(8,128)S(1)} copy-done((f32[96,128]{1,0:T(8,128)S(1)}, f32[96,128]{1,0:T(8,128)}, u32[]{:S(2)}) %copy-start) | copy-done | bytes 49176
  23.2 2.5 %columns.1 = (f32[264,128]{1,0:T(8,128)S(1)}, bf16[512,128]{1,0:T(8,128)(2,1)S(1)}) custom-call(f32[96,128]{1,0:T(8,128)S(1)} %copy-done, bf16[34,512,128]{2,1,0:T(8,128)(2,1)} %bitcast.25), custom_call_target="tpu_custom_call" | custom-call | flops 10000000 | bytes 4500000 | tf_op jit(solution)/shard_map/columns/pallas_call | solution.py:190
  25.7 0.1 collective-permute-start.4
  25.8 1.4 %collective-permute-start.5 = (f32[264,128]{1,0:T(8,128)S(1)}, f32[264,128]{1,0:T(8,128)S(1)}, u32[]{:S(2)}, u32[]{:S(2)}) collective-permute-start(f32[264,128]{1,0:T(8,128)S(1)} %get-tuple-element.13.s0), channel_id=1, source_target_pairs={{0,2},{1,3},{2,0},{3,1},{4,6},{5,7},{6,4},{7,5},{8,10},{9,11},{10,... | collective-permute-start | bytes 405512 | tf_op jit(solution)/shard_map/ppermute | solution.py:30
  27.2 0.0 collective-permute-done.1.t1
  27.2 0.7 %collective-permute-start.6 = (f32[264,128]{1,0:T(8,128)S(1)}, f32[264,128]{1,0:T(8,128)S(1)}, u32[]{:S(2)}, u32[]{:S(2)}) collective-permute-start(f32[264,128]{1,0:T(8,128)S(1)} %get-tuple-element.13.s0), channel_id=1, source_target_pairs={{0,3},{1,2},{2,1},{3,0},{4,7},{5,6},{6,5},{7,4},{8,11},{9,10},{10,... | collective-permute-start | bytes 405512 | tf_op jit(solution)/shard_map/ppermute | solution.py:30
  27.9 0.0 all-to-all-done
  27.9 0.0 collective-permute-done.2.t2
  27.9 0.0 collective-permute-done.3.t3
  27.9 0.3 pick.1
  28.2 11.3 %all_to_all.10 = f32[16,8,128]{2,1,0:T(8,128)S(1)} all-to-all(f32[16,8,128]{2,1,0:T(8,128)S(1)} %bitcast.24), channel_id=1, replica_groups=mesh['x'=4,'z'=4,'y'=4,'lev'=4] {'x','lev'}, dimensions={0} | all-to-all | bytes 131072 | tf_op jit(solution)/shard_map/all_to_all | solution.py:214
  39.5 0.0 copy-done.1
  39.5 3.7 %perturb.1 = (bf16[34,512,128]{2,1,0:T(8,128)(2,1)}, f32[128,128]{1,0:T(8,128)S(1)}) custom-call(f32[96,128]{1,0:T(8,128)S(1)} %copy-done.1, f32[128,128]{1,0:T(8,128)S(1)} %bitcast.22, bf16[512,128]{1,0:T(8,128)(2,1)S(1)} %get-tuple-element.10.place_ref, bf16[34,512,128]{2,1,0:T(8,128)(2,1)} %bitcast.26), custom_call_target="tpu_custom_call" | custom-call | flops 10000000 | bytes 9000000 | tf_op jit(solution)/shard_map/perturb/pallas_call | solution.py:216
  43.2 0.0 collective-permute-done.4.s1
  43.2 0.0 collective-permute-done.5.s2
  43.2 0.0 collective-permute-done.6.s3
  43.2 0.7 %integrals.1 = f32[256,128]{1,0:T(8,128)} custom-call(f32[128,128]{1,0:T(8,128)S(1)} %get-tuple-element.12.local_ref, f32[264,128]{1,0:T(8,128)S(1)} %get-tuple-element.13.s0, f32[264,128]{1,0:T(8,128)S(1)} %collective-permute-done.4.s1, f32[264,128]{1,0:T(8,128)S(1)} %collective-permute-done.5.s2, f32[264,128]{1,0:T(8,128)S(1)} %collective-permute-done.6.s3), custom_call_target="tpu_custom_call" | custom-call | tf_op jit(solution)/shard_map/integrals/pallas_call | solution.py:232
Async XLA Ops:
  0.6 11.0 %collective-permute-start = (f32[128,128]{1,0:T(8,128)}, f32[128,128]{1,0:T(8,128)S(1)}, u32[]{:S(2)}, u32[]{:S(2)}) collective-permute-start(f32[128,128]{1,0:T(8,128)} %param.5), channel_id=1, source_target_pairs={{0,0},{50,1},{17,2},{35,3},{16,16},{2,17},{33,18},{51,19},{32,32},... | collective-permute-start | bytes 196616 | tf_op jit(solution)/shard_map/ppermute | solution.py:22
  11.6 15.5 %collective-permute-start.1 = (f32[128,128]{1,0:T(8,128)S(1)}, f32[128,128]{1,0:T(8,128)S(1)}, u32[]{:S(2)}, u32[]{:S(2)}) collective-permute-start(f32[128,128]{1,0:T(8,128)S(1)} %collective-permute-done.t0), channel_id=1, source_target_pairs={{0,4},{4,8},{8,12},{12,0},{1,5},{5,9},{9,13},{13,1},{2,6},{6,10},{... | collective-permute-start | bytes 196616 | tf_op jit(solution)/shard_map/ppermute | solution.py:26
  12.9 14.9 %collective-permute-start.2 = (f32[128,128]{1,0:T(8,128)S(1)}, f32[128,128]{1,0:T(8,128)S(1)}, u32[]{:S(2)}, u32[]{:S(2)}) collective-permute-start(f32[128,128]{1,0:T(8,128)S(1)} %collective-permute-done.t0), channel_id=1, source_target_pairs={{0,8},{4,12},{8,0},{12,4},{1,9},{5,13},{9,1},{13,5},{2,10},{6,14},... | collective-permute-start | bytes 196616 | tf_op jit(solution)/shard_map/ppermute | solution.py:26
  15.6 12.3 %collective-permute-start.3 = (f32[128,128]{1,0:T(8,128)S(1)}, f32[128,128]{1,0:T(8,128)S(1)}, u32[]{:S(2)}, u32[]{:S(2)}) collective-permute-start(f32[128,128]{1,0:T(8,128)S(1)} %collective-permute-done.t0), channel_id=1, source_target_pairs={{0,12},{4,0},{8,4},{12,8},{1,13},{5,1},{9,5},{13,9},{2,14},{6,2},{... | collective-permute-start | bytes 196616 | tf_op jit(solution)/shard_map/ppermute | solution.py:26
  18.2 21.2 %copy-start.1 = (f32[96,128]{1,0:T(8,128)S(1)}, f32[96,128]{1,0:T(8,128)}, u32[]{:S(2)}) copy-start(f32[96,128]{1,0:T(8,128)} %get-tuple-element.8.scalars_ref) | copy-start | bytes 147460
  18.2 9.6 %all-to-all-start = ((s32[4,32,128]{2,1,0:T(8,128)}), s32[4,32,128]{2,1,0:T(8,128)S(1)}, u32[]{:S(2)}, u32[]{:S(2)}) async-start(s32[4,32,128]{2,1,0:T(8,128)} %bitcast.28), calls=%async_computation | async-start | bytes 131072 | tf_op jit(solution)/shard_map/all_to_all | solution.py:186
  22.4 0.8 %copy-start = (f32[96,128]{1,0:T(8,128)S(1)}, f32[96,128]{1,0:T(8,128)}, u32[]{:S(2)}) copy-start(f32[96,128]{1,0:T(8,128)} %get-tuple-element.8.scalars_ref) | copy-start | bytes 147460
  25.7 17.6 %collective-permute-start.4 = (f32[264,128]{1,0:T(8,128)S(1)}, f32[264,128]{1,0:T(8,128)S(1)}, u32[]{:S(2)}, u32[]{:S(2)}) collective-permute-start(f32[264,128]{1,0:T(8,128)S(1)} %get-tuple-element.13.s0), channel_id=1, source_target_pairs={{0,1},{1,0},{2,3},{3,2},{4,5},{5,4},{6,7},{7,6},{8,9},{9,8},{10,11... | collective-permute-start | bytes 405512 | tf_op jit(solution)/shard_map/ppermute | solution.py:30
  25.8 17.5 %collective-permute-start.5 = (f32[264,128]{1,0:T(8,128)S(1)}, f32[264,128]{1,0:T(8,128)S(1)}, u32[]{:S(2)}, u32[]{:S(2)}) collective-permute-start(f32[264,128]{1,0:T(8,128)S(1)} %get-tuple-element.13.s0), channel_id=1, source_target_pairs={{0,2},{1,3},{2,0},{3,1},{4,6},{5,7},{6,4},{7,5},{8,10},{9,11},{10,... | collective-permute-start | bytes 405512 | tf_op jit(solution)/shard_map/ppermute | solution.py:30
  27.2 16.1 %collective-permute-start.6 = (f32[264,128]{1,0:T(8,128)S(1)}, f32[264,128]{1,0:T(8,128)S(1)}, u32[]{:S(2)}, u32[]{:S(2)}) collective-permute-start(f32[264,128]{1,0:T(8,128)S(1)} %get-tuple-element.13.s0), channel_id=1, source_target_pairs={{0,3},{1,2},{2,1},{3,0},{4,7},{5,6},{6,5},{7,4},{8,11},{9,10},{10,... | collective-permute-start | bytes 405512 | tf_op jit(solution)/shard_map/ppermute | solution.py:30

commit v5 on v4

--- a/solution.py
+++ b/solution.py
@@ -26,6 +26,10 @@
     return lax.ppermute(a, "y", [(y, (y + step) % 4) for y in range(4)])
 
 
+def along_x(a, step):
+    return lax.ppermute(a, "x", [(x, (x + step) % 4) for x in range(4)])
+
+
 def across_lev(a, flip):
     return lax.ppermute(a, "lev", [(i, i ^ flip) for i in range(4)])
 
@@ -54,26 +58,22 @@
     return high, mid, low
 
 
-def request_kernel(source_ref, taper_ref, thick_ref, ids_ref, scalars_ref):
-    source = source_ref[...]
+def parts_of(source):
     band, row = source >> 7, source & 127
     offset = ((band >> 2) - lax.axis_index("z")) & 3
     lev = jnp.where(offset == 3, 1, jnp.where(offset == 0, 0, offset + 1))
-    table = (lax.axis_index("y") - band) & 3
-    holder = ((band >> 4) * 4 + lev) * 4 + table
+    return band >> 4, lev, (lax.axis_index("y") - band) & 3, row
+
+
+def prepare_kernel(source_ref, taper_ref, thick_ref, scalars_ref):
+    source = source_ref[...]
+    x, lev, table, _ = parts_of(source)
+    holder = (x * 4 + lev) * 4 + table
     member = iota((64, ROW), 0) == holder
     before = onehot(iota((ROW, ROW), 0) < iota((ROW, ROW), 1))
     count = dot(onehot(member), before)
     rank = jnp.sum(jnp.where(member, count, 0.0), axis=0, keepdims=True)
     pos = holder * 2 + rank.astype(jnp.int32)
-    slot = iota((ROW, ROW), 0)
-    asked = onehot(((slot >> 5) * 4 + lax.axis_index("lev")) * 8 + (slot & 7) == pos)
-
-    def everywhere(v):
-        return jnp.broadcast_to(v.astype(jnp.float32), (ROW, ROW)).astype(jnp.bfloat16)
-
-    ids = dot_nt(asked, everywhere(table)) * 128.0 + dot_nt(asked, everywhere(row))
-    ids_ref[...] = ids.astype(jnp.int32)
 
     taper, thick = taper_ref[...], thick_ref[...]
     levels = taper.shape[1]
@@ -86,7 +86,22 @@
     scalars_ref[0:LEVELS, :] = one_per_row(taper)
     scalars_ref[LEVELS : 2 * LEVELS, :] = one_per_row(taper * thick)
     scalars_ref[2 * LEVELS : 2 * LEVELS + 8, :] = jnp.broadcast_to(jnp.sum(thick * thick, axis=1, keepdims=True), (8, ROW))
-    scalars_ref[2 * LEVELS + 8 :, :] = jnp.broadcast_to(pos.astype(jnp.float32), (8, ROW))
+    scalars_ref[2 * LEVELS + 8 : 2 * LEVELS + 16, :] = jnp.broadcast_to(pos.astype(jnp.float32), (8, ROW))
+    scalars_ref[2 * LEVELS + 16 :, :] = jnp.broadcast_to(source.astype(jnp.float32), (8, ROW))
+
+
+def wanted_kernel(scalars_ref, from1, from2, from3, ids_ref):
+    slot = iota((ROW, ROW), 0)
+    step = (lax.axis_index("x") - (slot >> 5)) & 3
+    own = scalars_ref[2 * LEVELS + 16 : 2 * LEVELS + 17, :].astype(jnp.int32)
+    source = jnp.where(step == 0, own, jnp.where(step == 1, from1[...], jnp.where(step == 2, from2[...], from3[...])))
+    x, lev, table, row = parts_of(source)
+    mine = (x == lax.axis_index("x")) & (lev == lax.axis_index("lev")) & (table == ((slot >> 1) & 3))
+    before = onehot(iota((ROW, ROW), 0) < iota((ROW, ROW), 1))
+    count = dot(onehot(mine), before)
+    chosen = mine & (count == (slot & 1).astype(jnp.float32))
+    ids = jnp.sum(jnp.where(chosen, (table * ROW + row).astype(jnp.float32), 0.0), axis=1, keepdims=True)
+    ids_ref[...] = jnp.broadcast_to(ids, (ROW, ROW)).astype(jnp.int32)
 
 
 def pick_kernel(ids_ref, t0, t1, t2, t3, out_ref):
@@ -162,9 +177,13 @@
         store(i).wait()
 
 
-def integrals_kernel(local_ref, s0, s1, s2, s3, out_ref):
+def add_kernel(a_ref, b_ref, out_ref):
+    out_ref[...] = a_ref[...] + b_ref[...]
+
+
+def integrals_kernel(local_ref, s0, s1, out_ref):
     local = local_ref[...]
-    total = (s0[...] + s1[...]) + (s2[...] + s3[...])
+    total = s0[...] + s1[...]
     norm = jnp.sqrt(total[2 * ROW : 2 * ROW + 1, :])
     for k in range(2):
         out_ref[pl.ds(k, ROW, stride=2), :] = local * total[k * ROW : (k + 1) * ROW, :] / norm
@@ -176,15 +195,24 @@
     f32, s32 = jnp.float32, jnp.int32
 
     table = along_z(pattern)
-    ids, scalars = pl.pallas_call(
-        request_kernel,
-        out_shape=(jax.ShapeDtypeStruct((ROW, ROW), s32), jax.ShapeDtypeStruct((2 * LEVELS + 16, ROW), f32)),
-        in_specs=[vmem, vmem, vmem],
-        out_specs=(vmem, vmem),
-        name="request",
-    )(block_source.reshape(1, ROW), taper.reshape(1, levels), thickness.reshape(1, levels))
-    wanted = lax.all_to_all(ids.reshape(4, 32, ROW), "x", 0, 0, tiled=True).reshape(ROW, ROW)
+    source = block_source.reshape(1, ROW)
+    asked = [along_x(source, k) for k in (1, 2, 3)]
+    scalars = pl.pallas_call(
+        prepare_kernel,
+        out_shape=jax.ShapeDtypeStruct((2 * LEVELS + 24, ROW), f32),
+        in_specs=[vmem] * 3,
+        out_specs=vmem,
+        name="prepare",
+    )(source, taper.reshape(1, levels), thickness.reshape(1, levels))
     tables = [table] + [along_y(table, k) for k in (1, 2, 3)]
+    wanted = pl.pallas_call(
+        wanted_kernel,
+        out_shape=jax.ShapeDtypeStruct((ROW, ROW), s32),
+        in_specs=[vmem] * 4,
+        out_specs=vmem,
+        compiler_params=pltpu.CompilerParams(vmem_limit_bytes=4 << 20),
+        name="wanted",
+    )(scalars, *asked)
 
     x = tendencies.reshape(4, levels, ROW, ROW).transpose(1, 2, 0, 3).reshape(levels, 4 * ROW, ROW)
     sums, place = pl.pallas_call(
@@ -201,7 +229,16 @@
         compiler_params=pltpu.CompilerParams(vmem_limit_bytes=52 << 20),
         name="columns",
     )(scalars, x)
-    others = [across_lev(sums, flip) for flip in (1, 2, 3)]
+    pair = across_lev(sums, 1)
+    both = pl.pallas_call(
+        add_kernel,
+        out_shape=jax.ShapeDtypeStruct(sums.shape, f32),
+        in_specs=[vmem] * 2,
+        out_specs=vmem,
+        compiler_params=pltpu.CompilerParams(vmem_limit_bytes=4 << 20),
+        name="both",
+    )(sums, pair)
+    rest = across_lev(both, 2)
 
     picked = pl.pallas_call(
         pick_kernel,
@@ -232,11 +269,11 @@
     out = pl.pallas_call(
         integrals_kernel,
         out_shape=jax.ShapeDtypeStruct((2 * ROW, ROW), f32),
-        in_specs=[vmem] * 5,
+        in_specs=[vmem] * 3,
         out_specs=vmem,
         compiler_params=pltpu.CompilerParams(vmem_limit_bytes=4 << 20),
         name="integrals",
-    )(local, sums, *others)
+    )(local, both, rest)
     perturbed = y.reshape(levels, ROW, 4, ROW).transpose(2, 0, 1, 3).reshape(tendencies.shape)
     integrals = out.reshape(ROW, 2, ROW).transpose(1, 0, 2).reshape(2, ROW * ROW)
     return perturbed, integrals

time: 44.3 us -> 50.2 us (1.13)
  the two profiles are of different devices: /device:TPU:1 before, /device:TPU:65 now
where the time goes in v5:
time: 50.2 us; the launch traced here: 49.9 us
  starting transfers between devices  17 us (34%)
  blocking collectives  13.1 us (26%)
  waiting for transfers between devices  9.33 us (19%)
  Pallas kernels  8.95 us (18%)
  local copies, waits for them, and re-layouts  0.82 us (2%)
  between operations  0.71 us (1%)
    all_to_all x1, blocking collectives, program(): lax.all_to_all(picked.reshape(16, 8, ROW), ('x', 'lev'), 0, 0, tiled=True)  13.1 us
    ppermute x2, starting transfers between devices, across_lev(): return lax.ppermute(a, 'lev', [(i, i ^ flip) for i in range(4)])  5.82 us
    ppermute x3, waiting for transfers between devices, along_x(): return lax.ppermute(a, 'x', [(x, (x + step) % 4) for x in range(4)])  5.37 us
    ppermute x3, starting transfers between devices, along_y(): return lax.ppermute(a, 'y', [(y, (y + step) % 4) for y in range(4)])  4.7 us
    ppermute x3, starting transfers between devices, along_x(): return lax.ppermute(a, 'x', [(x, (x + step) % 4) for x in range(4)])  4.6 us
    ppermute x1, waiting for transfers between devices, along_z(): return lax.ppermute(a, ('z', 'lev'), pairs)  3.95 us
    pallas_call x1, Pallas kernels, program(): pl.pallas_call(perturb_kernel, out_shape=(jax.ShapeDtypeStruct(x.shape, x...  3.73 us
    pallas_call x1, Pallas kernels, program(): pl.pallas_call(column_kernel, out_shape=(jax.ShapeDtypeStruct((2 * ROW +...  2.48 us
  transfers between devices with their start and end apart: 9, of which 4 were waited for; matrix products, arithmetic and copies ran while one was open for 0% of the time, Pallas kernels for 9%

profile of v5, /device:TPU:65, one launch (start us, length us, event | category | flops | bytes accessed | tf_op | source)
XLA Modules:
  0.0 49.9 jit_solution(5534589949864464921)
XLA Ops:
  0.6 0.0 copy-start.1
  0.6 1.5 %prepare.1.scalars_ref = f32[104,128]{1,0:T(8,128)} custom-call(s32[1,128]{1,0:T(1,128)} %bitcast.27, f32[1,34]{1,0:T(1,128)} %bitcast.25, f32[1,34]{1,0:T(1,128)} %bitcast.26), custom_call_target="tpu_custom_call" | custom-call | tf_op jit(solution)/shard_map/prepare/pallas_call | solution.py:200
  2.1 0.0 copy-start
  2.1 0.8 %copy-done = f32[104,128]{1,0:T(8,128)S(1)} copy-done((f32[104,128]{1,0:T(8,128)S(1)}, f32[104,128]{1,0:T(8,128)}, u32[]{:S(2)}) %copy-start) | copy-done | bytes 53272
  2.9 0.0 copy-start.2
  3.0 2.5 %columns.1 = (f32[264,128]{1,0:T(8,128)S(1)}, bf16[512,128]{1,0:T(8,128)(2,1)S(1)}) custom-call(f32[104,128]{1,0:T(8,128)S(1)} %copy-done, bf16[34,512,128]{2,1,0:T(8,128)(2,1)} %bitcast.22), custom_call_target="tpu_custom_call" | custom-call | flops 10000000 | bytes 4500000 | tf_op jit(solution)/shard_map/columns/pallas_call | solution.py:218
  5.4 0.8 %collective-permute-start.7 = (f32[264,128]{1,0:T(8,128)S(1)}, f32[264,128]{1,0:T(8,128)S(1)}, u32[]{:S(2)}, u32[]{:S(2)}) collective-permute-start(f32[264,128]{1,0:T(8,128)S(1)} %get-tuple-element.9.a_ref), channel_id=1, source_target_pairs={{0,1},{1,0},{2,3},{3,2},{4,5},{5,4},{6,7},{7,6},{8,9},{9,8},{10,11... | collective-permute-start | bytes 405512 | tf_op jit(solution)/shard_map/ppermute | solution.py:34
  6.2 0.0 copy-done.2
  6.2 1.9 %collective-permute-start.3 = (f32[128,128]{1,0:T(8,128)S(1)}, f32[128,128]{1,0:T(8,128)S(1)}, u32[]{:S(2)}, u32[]{:S(2)}) collective-permute-start(f32[128,128]{1,0:T(8,128)S(1)} %copy-done.2), channel_id=1, source_target_pairs={{0,0},{50,1},{17,2},{35,3},{16,16},{2,17},{33,18},{51,19},{32,32},... | collective-permute-start | bytes 196616 | tf_op jit(solution)/shard_map/ppermute | solution.py:22
  8.1 3.9 %collective-permute-done.3.t0 = f32[128,128]{1,0:T(8,128)S(1)} collective-permute-done((f32[128,128]{1,0:T(8,128)S(1)}, f32[128,128]{1,0:T(8,128)S(1)}, u32[]{:S(2)}, u32[]{:S(2)}) %collective-permute-start.3) | collective-permute-done | bytes 65568 | tf_op jit(solution)/shard_map/ppermute | solution.py:22
  12.1 1.0 %collective-permute-start.4 = (f32[128,128]{1,0:T(8,128)S(1)}, f32[128,128]{1,0:T(8,128)S(1)}, u32[]{:S(2)}, u32[]{:S(2)}) collective-permute-start(f32[128,128]{1,0:T(8,128)S(1)} %collective-permute-done.3.t0), channel_id=1, source_target_pairs={{0,4},{4,8},{8,12},{12,0},{1,5},{5,9},{9,13},{13,1},{2,6},{6,10},{... | collective-permute-start | bytes 196616 | tf_op jit(solution)/shard_map/ppermute | solution.py:26
  13.1 2.9 %collective-permute-start.5 = (f32[128,128]{1,0:T(8,128)S(1)}, f32[128,128]{1,0:T(8,128)S(1)}, u32[]{:S(2)}, u32[]{:S(2)}) collective-permute-start(f32[128,128]{1,0:T(8,128)S(1)} %collective-permute-done.3.t0), channel_id=1, source_target_pairs={{0,8},{4,12},{8,0},{12,4},{1,9},{5,13},{9,1},{13,5},{2,10},{6,14},... | collective-permute-start | bytes 196616 | tf_op jit(solution)/shard_map/ppermute | solution.py:26
  16.0 0.8 %collective-permute-start.6 = (f32[128,128]{1,0:T(8,128)S(1)}, f32[128,128]{1,0:T(8,128)S(1)}, u32[]{:S(2)}, u32[]{:S(2)}) collective-permute-start(f32[128,128]{1,0:T(8,128)S(1)} %collective-permute-done.3.t0), channel_id=1, source_target_pairs={{0,12},{4,0},{8,4},{12,8},{1,13},{5,1},{9,5},{13,9},{2,14},{6,2},{... | collective-permute-start | bytes 196616 | tf_op jit(solution)/shard_map/ppermute | solution.py:26
  16.8 0.0 collective-permute-done.7.b_ref
  16.8 5.1 %collective-permute-start.8 = (f32[264,128]{1,0:T(8,128)S(1)}, f32[264,128]{1,0:T(8,128)S(1)}, u32[]{:S(2)}, u32[]{:S(2)}) collective-permute-start(f32[264,128]{1,0:T(8,128)S(1)} %both.1.s0), channel_id=1, source_target_pairs={{0,2},{1,3},{2,0},{3,1},{4,6},{5,7},{6,4},{7,5},{8,10},{9,11},{10,... | collective-permute-start | bytes 405512 | tf_op jit(solution)/shard_map/ppermute | solution.py:34
  21.8 0.0 copy-done.1
  21.8 1.2 %collective-permute-start = (s32[1,128]{1,0:T(1,128)S(1)}, s32[1,128]{1,0:T(1,128)S(1)}, u32[]{:S(2)}, u32[]{:S(2)}) collective-permute-start(s32[1,128]{1,0:T(1,128)S(1)} %bitcast.28), channel_id=1, source_target_pairs={{0,64},{64,128},{128,192},{192,0},{1,65},{65,129},{129,193},{193,1... | collective-permute-start | bytes 1544 | tf_op jit(solution)/shard_map/ppermute | solution.py:30
  23.1 2.4 %collective-permute-done.from1 = s32[1,128]{1,0:T(1,128)S(1)} collective-permute-done((s32[1,128]{1,0:T(1,128)S(1)}, s32[1,128]{1,0:T(1,128)S(1)}, u32[]{:S(2)}, u32[]{:S(2)}) %collective-permute-start) | collective-permute-done | bytes 544 | tf_op jit(solution)/shard_map/ppermute | solution.py:30
  25.5 1.8 %collective-permute-start.1 = (s32[1,128]{1,0:T(1,128)S(1)}, s32[1,128]{1,0:T(1,128)S(1)}, u32[]{:S(2)}, u32[]{:S(2)}) collective-permute-start(s32[1,128]{1,0:T(1,128)S(1)} %bitcast.29), channel_id=1, source_target_pairs={{0,128},{64,192},{128,0},{192,64},{1,129},{65,193},{129,1},{193,65... | collective-permute-start | bytes 1544 | tf_op jit(solution)/shard_map/ppermute | solution.py:30
  27.3 2.1 %collective-permute-done.1.from2 = s32[1,128]{1,0:T(1,128)S(1)} collective-permute-done((s32[1,128]{1,0:T(1,128)S(1)}, s32[1,128]{1,0:T(1,128)S(1)}, u32[]{:S(2)}, u32[]{:S(2)}) %collective-permute-start.1) | collective-permute-done | bytes 544 | tf_op jit(solution)/shard_map/ppermute | solution.py:30
  29.4 1.6 %collective-permute-start.2 = (s32[1,128]{1,0:T(1,128)S(1)}, s32[1,128]{1,0:T(1,128)S(1)}, u32[]{:S(2)}, u32[]{:S(2)}) collective-permute-start(s32[1,128]{1,0:T(1,128)S(1)} %bitcast.30), channel_id=1, source_target_pairs={{0,192},{64,0},{128,64},{192,128},{1,193},{65,1},{129,65},{193,129... | collective-permute-start | bytes 1544 | tf_op jit(solution)/shard_map/ppermute | solution.py:30
  31.0 0.9 %collective-permute-done.2.from3 = s32[1,128]{1,0:T(1,128)S(1)} collective-permute-done((s32[1,128]{1,0:T(1,128)S(1)}, s32[1,128]{1,0:T(1,128)S(1)}, u32[]{:S(2)}, u32[]{:S(2)}) %collective-permute-start.2) | collective-permute-done | bytes 544 | tf_op jit(solution)/shard_map/ppermute | solution.py:30
  31.8 0.3 wanted.1.ids_ref
  32.1 0.0 collective-permute-done.4.t1
  32.1 0.0 collective-permute-done.5.t2
  32.1 0.0 collective-permute-done.6.t3
  32.1 0.3 pick.1
  32.4 13.1 %all_to_all.5 = f32[16,8,128]{2,1,0:T(8,128)S(1)} all-to-all(f32[16,8,128]{2,1,0:T(8,128)S(1)} %bitcast.21), channel_id=1, replica_groups=mesh['x'=4,'z'=4,'y'=4,'lev'=4] {'x','lev'}, dimensions={0} | all-to-all | bytes 131072 | tf_op jit(solution)/shard_map/all_to_all | solution.py:251
  45.5 3.7 %perturb.1 = (bf16[34,512,128]{2,1,0:T(8,128)(2,1)}, f32[128,128]{1,0:T(8,128)S(1)}) custom-call(f32[104,128]{1,0:T(8,128)S(1)} %copy-done, f32[128,128]{1,0:T(8,128)S(1)} %bitcast.20, bf16[512,128]{1,0:T(8,128)(2,1)S(1)} %get-tuple-element.6.place_ref, bf16[34,512,128]{2,1,0:T(8,128)(2,1)} %bitcast.23), custom_call_target="tpu_custom_call" | custom-call | flops 10000000 | bytes 9000000 | tf_op jit(solution)/shard_map/perturb/pallas_call | solution.py:253
  49.2 0.0 collective-permute-done.8.s1
  49.2 0.7 %integrals.1 = f32[256,128]{1,0:T(8,128)} custom-call(f32[128,128]{1,0:T(8,128)S(1)} %get-tuple-element.8.local_ref, f32[264,128]{1,0:T(8,128)S(1)} %both.1.s0, f32[264,128]{1,0:T(8,128)S(1)} %collective-permute-done.8.s1), custom_call_target="tpu_custom_call" | custom-call | tf_op jit(solution)/shard_map/integrals/pallas_call | solution.py:269
  (1 shorter events, 0.0 us)
Async XLA Ops:
  0.6 21.2 %copy-start.1 = (s32[128]{0:T(128)S(1)}, s32[128]{0:T(128)}, u32[]{:S(2)}) copy-start(s32[128]{0:T(128)} %param.8) | copy-start | bytes 1540
  2.1 0.8 %copy-start = (f32[104,128]{1,0:T(8,128)S(1)}, f32[104,128]{1,0:T(8,128)}, u32[]{:S(2)}) copy-start(f32[104,128]{1,0:T(8,128)} %prepare.1.scalars_ref) | copy-start | bytes 159748
  2.9 3.3 %copy-start.2 = (f32[128,128]{1,0:T(8,128)S(1)}, f32[128,128]{1,0:T(8,128)}, u32[]{:S(2)}) copy-start(f32[128,128]{1,0:T(8,128)} %param.5) | copy-start | bytes 196612
  5.4 11.3 %collective-permute-start.7 = (f32[264,128]{1,0:T(8,128)S(1)}, f32[264,128]{1,0:T(8,128)S(1)}, u32[]{:S(2)}, u32[]{:S(2)}) collective-permute-start(f32[264,128]{1,0:T(8,128)S(1)} %get-tuple-element.9.a_ref), channel_id=1, source_target_pairs={{0,1},{1,0},{2,3},{3,2},{4,5},{5,4},{6,7},{7,6},{8,9},{9,8},{10,11... | collective-permute-start | bytes 405512 | tf_op jit(solution)/shard_map/ppermute | solution.py:34
  6.2 5.9 %collective-permute-start.3 = (f32[128,128]{1,0:T(8,128)S(1)}, f32[128,128]{1,0:T(8,128)S(1)}, u32[]{:S(2)}, u32[]{:S(2)}) collective-permute-start(f32[128,128]{1,0:T(8,128)S(1)} %copy-done.2), channel_id=1, source_target_pairs={{0,0},{50,1},{17,2},{35,3},{16,16},{2,17},{33,18},{51,19},{32,32},... | collective-permute-start | bytes 196616 | tf_op jit(solution)/shard_map/ppermute | solution.py:22
  12.1 20.0 %collective-permute-start.4 = (f32[128,128]{1,0:T(8,128)S(1)}, f32[128,128]{1,0:T(8,128)S(1)}, u32[]{:S(2)}, u32[]{:S(2)}) collective-permute-start(f32[128,128]{1,0:T(8,128)S(1)} %collective-permute-done.3.t0), channel_id=1, source_target_pairs={{0,4},{4,8},{8,12},{12,0},{1,5},{5,9},{9,13},{13,1},{2,6},{6,10},{... | collective-permute-start | bytes 196616 | tf_op jit(solution)/shard_map/ppermute | solution.py:26
  13.1 19.0 %collective-permute-start.5 = (f32[128,128]{1,0:T(8,128)S(1)}, f32[128,128]{1,0:T(8,128)S(1)}, u32[]{:S(2)}, u32[]{:S(2)}) collective-permute-start(f32[128,128]{1,0:T(8,128)S(1)} %collective-permute-done.3.t0), channel_id=1, source_target_pairs={{0,8},{4,12},{8,0},{12,4},{1,9},{5,13},{9,1},{13,5},{2,10},{6,14},... | collective-permute-start | bytes 196616 | tf_op jit(solution)/shard_map/ppermute | solution.py:26
  16.0 16.1 %collective-permute-start.6 = (f32[128,128]{1,0:T(8,128)S(1)}, f32[128,128]{1,0:T(8,128)S(1)}, u32[]{:S(2)}, u32[]{:S(2)}) collective-permute-start(f32[128,128]{1,0:T(8,128)S(1)} %collective-permute-done.3.t0), channel_id=1, source_target_pairs={{0,12},{4,0},{8,4},{12,8},{1,13},{5,1},{9,5},{13,9},{2,14},{6,2},{... | collective-permute-start | bytes 196616 | tf_op jit(solution)/shard_map/ppermute | solution.py:26
  16.8 32.4 %collective-permute-start.8 = (f32[264,128]{1,0:T(8,128)S(1)}, f32[264,128]{1,0:T(8,128)S(1)}, u32[]{:S(2)}, u32[]{:S(2)}) collective-permute-start(f32[264,128]{1,0:T(8,128)S(1)} %both.1.s0), channel_id=1, source_target_pairs={{0,2},{1,3},{2,0},{3,1},{4,6},{5,7},{6,4},{7,5},{8,10},{9,11},{10,... | collective-permute-start | bytes 405512 | tf_op jit(solution)/shard_map/ppermute | solution.py:34
  21.8 3.6 %collective-permute-start = (s32[1,128]{1,0:T(1,128)S(1)}, s32[1,128]{1,0:T(1,128)S(1)}, u32[]{:S(2)}, u32[]{:S(2)}) collective-permute-start(s32[1,128]{1,0:T(1,128)S(1)} %bitcast.28), channel_id=1, source_target_pairs={{0,64},{64,128},{128,192},{192,0},{1,65},{65,129},{129,193},{193,1... | collective-permute-start | bytes 1544 | tf_op jit(solution)/shard_map/ppermute | solution.py:30
  25.5 3.9 %collective-permute-start.1 = (s32[1,128]{1,0:T(1,128)S(1)}, s32[1,128]{1,0:T(1,128)S(1)}, u32[]{:S(2)}, u32[]{:S(2)}) collective-permute-start(s32[1,128]{1,0:T(1,128)S(1)} %bitcast.29), channel_id=1, source_target_pairs={{0,128},{64,192},{128,0},{192,64},{1,129},{65,193},{129,1},{193,65... | collective-permute-start | bytes 1544 | tf_op jit(solution)/shard_map/ppermute | solution.py:30
  29.4 2.4 %collective-permute-start.2 = (s32[1,128]{1,0:T(1,128)S(1)}, s32[1,128]{1,0:T(1,128)S(1)}, u32[]{:S(2)}, u32[]{:S(2)}) collective-permute-start(s32[1,128]{1,0:T(1,128)S(1)} %bitcast.30), channel_id=1, source_target_pairs={{0,192},{64,0},{128,64},{192,128},{1,193},{65,1},{129,65},{193,129... | collective-permute-start | bytes 1544 | tf_op jit(solution)/shard_map/ppermute | solution.py:30

commit v6 on v5

--- a/solution.py
+++ b/solution.py
@@ -12,6 +12,7 @@
 LEVELS = 40
 PARTS = 8
 PART = 4 * ROW // PARTS
+HEAD = 22
 
 
 def along_z(a):
@@ -114,31 +115,38 @@
     out_ref[...] = (total[0] + total[1]) + total[2]
 
 
-def fetches(x_hbm, x_ref, sems):
-    def fetch(i):
+def fetches(pieces):
+    def copies(i):
         rows = pl.ds(pl.multiple_of(i * PART, PART), PART)
-        return pltpu.make_async_copy(x_hbm.at[:, rows, :], x_ref.at[:, rows, :], sems.at[i])
+        return [pltpu.make_async_copy(a.at[:, rows, :], b.at[:, rows, :], sems.at[i]) for a, b, sems in pieces]
 
     for i in range(PARTS):
-        fetch(i).start()
-    return fetch
-
-
-def column_kernel(scalars_ref, x_hbm, sums_ref, place_ref, acc_ref, x_ref, sems):
-    levels = x_ref.shape[0]
-    fetch = fetches(x_hbm, x_ref, sems)
+        for copy in copies(i):
+            copy.start()
+
+    def wait(i):
+        for copy in copies(i):
+            copy.wait()
+
+    return wait
+
+
+def column_kernel(scalars_ref, x_hbm, sums_ref, place_ref, head_ref, acc_ref, tail_ref, head_sems, sems):
+    levels = x_hbm.shape[0]
+    wait = fetches([(x_hbm.at[:HEAD], head_ref, head_sems), (x_hbm.at[HEAD:], tail_ref, sems)])
     pos = jnp.broadcast_to(scalars_ref[2 * LEVELS + 8 : 2 * LEVELS + 9, :], (ROW, ROW)).astype(jnp.bfloat16)
     expand = onehot(iota((4 * ROW, ROW), 0) >> 2 == iota((4 * ROW, ROW), 1))
     slot = dot_nt(expand, pos).astype(jnp.int32)
     place_ref[...] = onehot(slot == iota((4 * ROW, ROW), 1))
 
     def chunk(i, carry):
-        fetch(i).wait()
+        wait(i)
         for r in range(0, PART, 64):
             rows = pl.ds(pl.multiple_of(i * PART + r, 64), 64)
-            acc = x_ref[0, rows, :].astype(jnp.float32) * scalars_ref[LEVELS : LEVELS + 1, :]
+            acc = head_ref[0, rows, :].astype(jnp.float32) * scalars_ref[LEVELS : LEVELS + 1, :]
             for l in range(1, levels):
-                acc = acc + x_ref[l, rows, :].astype(jnp.float32) * scalars_ref[LEVELS + l : LEVELS + l + 1, :]
+                here = head_ref[l, rows, :] if l < HEAD else tail_ref[l - HEAD, rows, :]
+                acc = acc + here.astype(jnp.float32) * scalars_ref[LEVELS + l : LEVELS + l + 1, :]
             acc_ref[rows, :] = acc
         return carry
 
@@ -148,9 +156,9 @@
     sums_ref[pl.ds(2 * ROW, 8), :] = scalars_ref[2 * LEVELS : 2 * LEVELS + 8, :]
 
 
-def perturb_kernel(scalars_ref, arrived_ref, place_ref, x_hbm, y_hbm, clipped_ref, local_ref, x_ref, y_ref, in_sems, sems):
-    levels = x_ref.shape[0]
-    fetch = fetches(x_hbm, x_ref, in_sems)
+def perturb_kernel(scalars_ref, arrived_ref, place_ref, head_ref, x_hbm, y_hbm, clipped_ref, local_ref, x_ref, y_ref, in_sems, sems):
+    levels = y_ref.shape[0]
+    wait = fetches([(x_hbm.at[HEAD:], x_ref, in_sems)])
     parts = three_parts(jnp.tanh(arrived_ref[...]))
     place = place_ref[...]
     local_ref[...] = (dot(place, parts[0]) + dot(place, parts[1])) + dot(place, parts[2])
@@ -160,13 +168,14 @@
         return pltpu.make_async_copy(y_ref.at[:, rows, :], y_hbm.at[:, rows, :], sems.at[i])
 
     def chunk(i, carry):
-        fetch(i).wait()
+        wait(i)
         for r in range(0, PART, 32):
             rows = pl.ds(pl.multiple_of(i * PART + r, 32), 32)
             local = local_ref[rows, :]
             for l in range(levels):
                 scale = 1.0 + scalars_ref[l : l + 1, :] * local
-                y_ref[l, rows, :] = (x_ref[l, rows, :].astype(jnp.float32) * scale).astype(jnp.bfloat16)
+                here = head_ref[l, rows, :] if l < HEAD else x_ref[l - HEAD, rows, :]
+                y_ref[l, rows, :] = (here.astype(jnp.float32) * scale).astype(jnp.bfloat16)
         store(i).start()
         return carry
 
@@ -215,18 +224,23 @@
     )(scalars, *asked)
 
     x = tendencies.reshape(4, levels, ROW, ROW).transpose(1, 2, 0, 3).reshape(levels, 4 * ROW, ROW)
-    sums, place = pl.pallas_call(
+    sums, place, head = pl.pallas_call(
         column_kernel,
-        out_shape=(jax.ShapeDtypeStruct((2 * ROW + 8, ROW), f32), jax.ShapeDtypeStruct((4 * ROW, ROW), jnp.bfloat16)),
+        out_shape=(
+            jax.ShapeDtypeStruct((2 * ROW + 8, ROW), f32),
+            jax.ShapeDtypeStruct((4 * ROW, ROW), jnp.bfloat16),
+            jax.ShapeDtypeStruct((HEAD, 4 * ROW, ROW), x.dtype),
+        ),
         in_specs=[vmem, hbm],
-        out_specs=(vmem, vmem),
+        out_specs=(vmem, vmem, vmem),
         scratch_shapes=[
             pltpu.VMEM((4 * ROW, ROW), f32),
-            pltpu.VMEM(x.shape, x.dtype),
+            pltpu.VMEM((levels - HEAD, 4 * ROW, ROW), x.dtype),
+            pltpu.SemaphoreType.DMA((PARTS,)),
             pltpu.SemaphoreType.DMA((PARTS,)),
         ],
         cost_estimate=pl.CostEstimate(flops=10_000_000, bytes_accessed=4_500_000, transcendentals=0),
-        compiler_params=pltpu.CompilerParams(vmem_limit_bytes=52 << 20),
+        compiler_params=pltpu.CompilerParams(vmem_limit_bytes=50 << 20),
         name="columns",
     )(scalars, x)
     pair = across_lev(sums, 1)
@@ -253,19 +267,19 @@
     y, local = pl.pallas_call(
         perturb_kernel,
         out_shape=(jax.ShapeDtypeStruct(x.shape, x.dtype), jax.ShapeDtypeStruct((ROW, ROW), f32)),
-        in_specs=[vmem, vmem, vmem, hbm],
+        in_specs=[vmem, vmem, vmem, vmem, hbm],
         out_specs=(hbm, vmem),
         scratch_shapes=[
             pltpu.VMEM((4 * ROW, ROW), f32),
-            pltpu.VMEM(x.shape, x.dtype),
+            pltpu.VMEM((levels - HEAD, 4 * ROW, ROW), x.dtype),
             pltpu.VMEM(x.shape, x.dtype),
             pltpu.SemaphoreType.DMA((PARTS,)),
             pltpu.SemaphoreType.DMA((PARTS,)),
         ],
         cost_estimate=pl.CostEstimate(flops=10_000_000, bytes_accessed=9_000_000, transcendentals=0),
-        compiler_params=pltpu.CompilerParams(vmem_limit_bytes=52 << 20),
+        compiler_params=pltpu.CompilerParams(vmem_limit_bytes=50 << 20),
         name="perturb",
-    )(scalars, arrived, place, x)
+    )(scalars, arrived, place, head, x)
     out = pl.pallas_call(
         integrals_kernel,
         out_shape=jax.ShapeDtypeStruct((2 * ROW, ROW), f32),

time: 50.2 us -> 49.9 us (level)
  transfers between devices with their start and end apart: 9 -> 9, of which waited for: 4 -> 4; matrix products, arithmetic and copies ran while one was open for 0% -> 0% of each run, Pallas kernels for 9% -> 8%
where the time goes in v6:
time: 49.9 us; the launch traced here: 49.7 us
  starting transfers between devices  17 us (34%)
  blocking collectives  13.1 us (26%)
  waiting for transfers between devices  9.33 us (19%)
  Pallas kernels  8.69 us (17%)
  local copies, waits for them, and re-layouts  0.82 us (2%)
  between operations  0.71 us (1%)
    all_to_all x1, blocking collectives, program(): lax.all_to_all(picked.reshape(16, 8, ROW), ('x', 'lev'), 0, 0, tiled=True)  13.1 us
    ppermute x2, starting transfers between devices, across_lev(): return lax.ppermute(a, 'lev', [(i, i ^ flip) for i in range(4)])  5.82 us
    ppermute x3, waiting for transfers between devices, along_x(): return lax.ppermute(a, 'x', [(x, (x + step) % 4) for x in range(4)])  5.37 us
    ppermute x3, starting transfers between devices, along_y(): return lax.ppermute(a, 'y', [(y, (y + step) % 4) for y in range(4)])  4.7 us
    ppermute x3, starting transfers between devices, along_x(): return lax.ppermute(a, 'x', [(x, (x + step) % 4) for x in range(4)])  4.6 us
    ppermute x1, waiting for transfers between devices, along_z(): return lax.ppermute(a, ('z', 'lev'), pairs)  3.95 us
    pallas_call x1, Pallas kernels, program(): pl.pallas_call(perturb_kernel, out_shape=(jax.ShapeDtypeStruct(x.shape, x...  3.39 us
    pallas_call x1, Pallas kernels, program(): pl.pallas_call(column_kernel, out_shape=(jax.ShapeDtypeStruct((2 * ROW +...  2.57 us
  transfers between devices with their start and end apart: 9, of which 4 were waited for; matrix products, arithmetic and copies ran while one was open for 0% of the time, Pallas kernels for 8%

profile of v6, /device:TPU:65, one launch (start us, length us, event | category | flops | bytes accessed | tf_op | source)
XLA Modules:
  0.0 49.7 jit_solution(7323955696124498635)
XLA Ops:
  0.6 0.0 copy-start.1
  0.6 1.5 %prepare.1.scalars_ref = f32[104,128]{1,0:T(8,128)} custom-call(s32[1,128]{1,0:T(1,128)} %bitcast.27, f32[1,34]{1,0:T(1,128)} %bitcast.25, f32[1,34]{1,0:T(1,128)} %bitcast.26), custom_call_target="tpu_custom_call" | custom-call | tf_op jit(solution)/shard_map/prepare/pallas_call | solution.py:209
  2.1 0.0 copy-start
  2.1 0.8 %copy-done = f32[104,128]{1,0:T(8,128)S(1)} copy-done((f32[104,128]{1,0:T(8,128)S(1)}, f32[104,128]{1,0:T(8,128)}, u32[]{:S(2)}) %copy-start) | copy-done | bytes 53272
  2.9 0.0 copy-start.2
  3.0 2.6 %columns.1 = (f32[264,128]{1,0:T(8,128)S(1)}, bf16[512,128]{1,0:T(8,128)(2,1)S(1)}, bf16[22,512,128]{2,1,0:T(8,128)(2,1)S(1)}) custom-call(f32[104,128]{1,0:T(8,128)S(1)} %copy-done, bf16[34,512,128]{2,1,0:T(8,128)(2,1)} %bitcast.22), custom_call_target="tpu_custom_call" | custom-call | flops 10000000 | bytes 4500000 | tf_op jit(solution)/shard_map/columns/pallas_call | solution.py:227
  5.5 0.8 %collective-permute-start.7 = (f32[264,128]{1,0:T(8,128)S(1)}, f32[264,128]{1,0:T(8,128)S(1)}, u32[]{:S(2)}, u32[]{:S(2)}) collective-permute-start(f32[264,128]{1,0:T(8,128)S(1)} %get-tuple-element.11.a_ref), channel_id=1, source_target_pairs={{0,1},{1,0},{2,3},{3,2},{4,5},{5,4},{6,7},{7,6},{8,9},{9,8},{10,11... | collective-permute-start | bytes 405512 | tf_op jit(solution)/shard_map/ppermute | solution.py:35
  6.3 0.0 copy-done.2
  6.3 1.9 %collective-permute-start.3 = (f32[128,128]{1,0:T(8,128)S(1)}, f32[128,128]{1,0:T(8,128)S(1)}, u32[]{:S(2)}, u32[]{:S(2)}) collective-permute-start(f32[128,128]{1,0:T(8,128)S(1)} %copy-done.2), channel_id=1, source_target_pairs={{0,0},{50,1},{17,2},{35,3},{16,16},{2,17},{33,18},{51,19},{32,32},... | collective-permute-start | bytes 196616 | tf_op jit(solution)/shard_map/ppermute | solution.py:23
  8.2 3.9 %collective-permute-done.3.t0 = f32[128,128]{1,0:T(8,128)S(1)} collective-permute-done((f32[128,128]{1,0:T(8,128)S(1)}, f32[128,128]{1,0:T(8,128)S(1)}, u32[]{:S(2)}, u32[]{:S(2)}) %collective-permute-start.3) | collective-permute-done | bytes 65568 | tf_op jit(solution)/shard_map/ppermute | solution.py:23
  12.2 1.0 %collective-permute-start.4 = (f32[128,128]{1,0:T(8,128)S(1)}, f32[128,128]{1,0:T(8,128)S(1)}, u32[]{:S(2)}, u32[]{:S(2)}) collective-permute-start(f32[128,128]{1,0:T(8,128)S(1)} %collective-permute-done.3.t0), channel_id=1, source_target_pairs={{0,4},{4,8},{8,12},{12,0},{1,5},{5,9},{9,13},{13,1},{2,6},{6,10},{... | collective-permute-start | bytes 196616 | tf_op jit(solution)/shard_map/ppermute | solution.py:27
  13.2 2.9 %collective-permute-start.5 = (f32[128,128]{1,0:T(8,128)S(1)}, f32[128,128]{1,0:T(8,128)S(1)}, u32[]{:S(2)}, u32[]{:S(2)}) collective-permute-start(f32[128,128]{1,0:T(8,128)S(1)} %collective-permute-done.3.t0), channel_id=1, source_target_pairs={{0,8},{4,12},{8,0},{12,4},{1,9},{5,13},{9,1},{13,5},{2,10},{6,14},... | collective-permute-start | bytes 196616 | tf_op jit(solution)/shard_map/ppermute | solution.py:27
  16.1 0.8 %collective-permute-start.6 = (f32[128,128]{1,0:T(8,128)S(1)}, f32[128,128]{1,0:T(8,128)S(1)}, u32[]{:S(2)}, u32[]{:S(2)}) collective-permute-start(f32[128,128]{1,0:T(8,128)S(1)} %collective-permute-done.3.t0), channel_id=1, source_target_pairs={{0,12},{4,0},{8,4},{12,8},{1,13},{5,1},{9,5},{13,9},{2,14},{6,2},{... | collective-permute-start | bytes 196616 | tf_op jit(solution)/shard_map/ppermute | solution.py:27
  16.9 0.0 collective-permute-done.7.b_ref
  16.9 5.1 %collective-permute-start.8 = (f32[264,128]{1,0:T(8,128)S(1)}, f32[264,128]{1,0:T(8,128)S(1)}, u32[]{:S(2)}, u32[]{:S(2)}) collective-permute-start(f32[264,128]{1,0:T(8,128)S(1)} %both.1.s0), channel_id=1, source_target_pairs={{0,2},{1,3},{2,0},{3,1},{4,6},{5,7},{6,4},{7,5},{8,10},{9,11},{10,... | collective-permute-start | bytes 405512 | tf_op jit(solution)/shard_map/ppermute | solution.py:35
  21.9 0.0 copy-done.1
  21.9 1.2 %collective-permute-start = (s32[1,128]{1,0:T(1,128)S(1)}, s32[1,128]{1,0:T(1,128)S(1)}, u32[]{:S(2)}, u32[]{:S(2)}) collective-permute-start(s32[1,128]{1,0:T(1,128)S(1)} %bitcast.28), channel_id=1, source_target_pairs={{0,64},{64,128},{128,192},{192,0},{1,65},{65,129},{129,193},{193,1... | collective-permute-start | bytes 1544 | tf_op jit(solution)/shard_map/ppermute | solution.py:31
  23.1 2.4 %collective-permute-done.from1 = s32[1,128]{1,0:T(1,128)S(1)} collective-permute-done((s32[1,128]{1,0:T(1,128)S(1)}, s32[1,128]{1,0:T(1,128)S(1)}, u32[]{:S(2)}, u32[]{:S(2)}) %collective-permute-start) | collective-permute-done | bytes 544 | tf_op jit(solution)/shard_map/ppermute | solution.py:31
  25.6 1.8 %collective-permute-start.1 = (s32[1,128]{1,0:T(1,128)S(1)}, s32[1,128]{1,0:T(1,128)S(1)}, u32[]{:S(2)}, u32[]{:S(2)}) collective-permute-start(s32[1,128]{1,0:T(1,128)S(1)} %bitcast.29), channel_id=1, source_target_pairs={{0,128},{64,192},{128,0},{192,64},{1,129},{65,193},{129,1},{193,65... | collective-permute-start | bytes 1544 | tf_op jit(solution)/shard_map/ppermute | solution.py:31
  27.4 2.1 %collective-permute-done.1.from2 = s32[1,128]{1,0:T(1,128)S(1)} collective-permute-done((s32[1,128]{1,0:T(1,128)S(1)}, s32[1,128]{1,0:T(1,128)S(1)}, u32[]{:S(2)}, u32[]{:S(2)}) %collective-permute-start.1) | collective-permute-done | bytes 544 | tf_op jit(solution)/shard_map/ppermute | solution.py:31
  29.5 1.6 %collective-permute-start.2 = (s32[1,128]{1,0:T(1,128)S(1)}, s32[1,128]{1,0:T(1,128)S(1)}, u32[]{:S(2)}, u32[]{:S(2)}) collective-permute-start(s32[1,128]{1,0:T(1,128)S(1)} %bitcast.30), channel_id=1, source_target_pairs={{0,192},{64,0},{128,64},{192,128},{1,193},{65,1},{129,65},{193,129... | collective-permute-start | bytes 1544 | tf_op jit(solution)/shard_map/ppermute | solution.py:31
  31.1 0.9 %collective-permute-done.2.from3 = s32[1,128]{1,0:T(1,128)S(1)} collective-permute-done((s32[1,128]{1,0:T(1,128)S(1)}, s32[1,128]{1,0:T(1,128)S(1)}, u32[]{:S(2)}, u32[]{:S(2)}) %collective-permute-start.2) | collective-permute-done | bytes 544 | tf_op jit(solution)/shard_map/ppermute | solution.py:31
  31.9 0.3 wanted.1.ids_ref
  32.2 0.0 collective-permute-done.4.t1
  32.2 0.0 collective-permute-done.5.t2
  32.2 0.0 collective-permute-done.6.t3
  32.2 0.3 pick.1
  32.5 13.1 %all_to_all.5 = f32[16,8,128]{2,1,0:T(8,128)S(1)} all-to-all(f32[16,8,128]{2,1,0:T(8,128)S(1)} %bitcast.21), channel_id=1, replica_groups=mesh['x'=4,'z'=4,'y'=4,'lev'=4] {'x','lev'}, dimensions={0} | all-to-all | bytes 131072 | tf_op jit(solution)/shard_map/all_to_all | solution.py:265
  45.6 3.4 %perturb.1 = (bf16[34,512,128]{2,1,0:T(8,128)(2,1)}, f32[128,128]{1,0:T(8,128)S(1)}) custom-call(f32[104,128]{1,0:T(8,128)S(1)} %copy-done, f32[128,128]{1,0:T(8,128)S(1)} %bitcast.20, bf16[512,128]{1,0:T(8,128)(2,1)S(1)} %get-tuple-element.7.place_ref, bf16[22,512,128]{2,1,0:T(8,128)(2,1)S(1)} %get-tuple-element.8.head_ref, bf16[34,512,128]{2,1,0:T(8,128)(2,1)} %bitcast.23), custom_call_target="tpu_custom_call" | custom-call | flops 10000000 | bytes 9000000 | tf_op jit(solution)/shard_map/perturb/pallas_call | solution.py:267
  49.0 0.0 collective-permute-done.8.s1
  49.0 0.7 %integrals.1 = f32[256,128]{1,0:T(8,128)} custom-call(f32[128,128]{1,0:T(8,128)S(1)} %get-tuple-element.10.local_ref, f32[264,128]{1,0:T(8,128)S(1)} %both.1.s0, f32[264,128]{1,0:T(8,128)S(1)} %collective-permute-done.8.s1), custom_call_target="tpu_custom_call" | custom-call | tf_op jit(solution)/shard_map/integrals/pallas_call | solution.py:283
  (1 shorter events, 0.0 us)
Async XLA Ops:
  0.6 21.3 %copy-start.1 = (s32[128]{0:T(128)S(1)}, s32[128]{0:T(128)}, u32[]{:S(2)}) copy-start(s32[128]{0:T(128)} %param.8) | copy-start | bytes 1540
  2.1 0.8 %copy-start = (f32[104,128]{1,0:T(8,128)S(1)}, f32[104,128]{1,0:T(8,128)}, u32[]{:S(2)}) copy-start(f32[104,128]{1,0:T(8,128)} %prepare.1.scalars_ref) | copy-start | bytes 159748
  2.9 3.3 %copy-start.2 = (f32[128,128]{1,0:T(8,128)S(1)}, f32[128,128]{1,0:T(8,128)}, u32[]{:S(2)}) copy-start(f32[128,128]{1,0:T(8,128)} %param.5) | copy-start | bytes 196612
  5.5 11.3 %collective-permute-start.7 = (f32[264,128]{1,0:T(8,128)S(1)}, f32[264,128]{1,0:T(8,128)S(1)}, u32[]{:S(2)}, u32[]{:S(2)}) collective-permute-start(f32[264,128]{1,0:T(8,128)S(1)} %get-tuple-element.11.a_ref), channel_id=1, source_target_pairs={{0,1},{1,0},{2,3},{3,2},{4,5},{5,4},{6,7},{7,6},{8,9},{9,8},{10,11... | collective-permute-start | bytes 405512 | tf_op jit(solution)/shard_map/ppermute | solution.py:35
  6.3 5.9 %collective-permute-start.3 = (f32[128,128]{1,0:T(8,128)S(1)}, f32[128,128]{1,0:T(8,128)S(1)}, u32[]{:S(2)}, u32[]{:S(2)}) collective-permute-start(f32[128,128]{1,0:T(8,128)S(1)} %copy-done.2), channel_id=1, source_target_pairs={{0,0},{50,1},{17,2},{35,3},{16,16},{2,17},{33,18},{51,19},{32,32},... | collective-permute-start | bytes 196616 | tf_op jit(solution)/shard_map/ppermute | solution.py:23
  12.2 20.0 %collective-permute-start.4 = (f32[128,128]{1,0:T(8,128)S(1)}, f32[128,128]{1,0:T(8,128)S(1)}, u32[]{:S(2)}, u32[]{:S(2)}) collective-permute-start(f32[128,128]{1,0:T(8,128)S(1)} %collective-permute-done.3.t0), channel_id=1, source_target_pairs={{0,4},{4,8},{8,12},{12,0},{1,5},{5,9},{9,13},{13,1},{2,6},{6,10},{... | collective-permute-start | bytes 196616 | tf_op jit(solution)/shard_map/ppermute | solution.py:27
  13.2 19.0 %collective-permute-start.5 = (f32[128,128]{1,0:T(8,128)S(1)}, f32[128,128]{1,0:T(8,128)S(1)}, u32[]{:S(2)}, u32[]{:S(2)}) collective-permute-start(f32[128,128]{1,0:T(8,128)S(1)} %collective-permute-done.3.t0), channel_id=1, source_target_pairs={{0,8},{4,12},{8,0},{12,4},{1,9},{5,13},{9,1},{13,5},{2,10},{6,14},... | collective-permute-start | bytes 196616 | tf_op jit(solution)/shard_map/ppermute | solution.py:27
  16.1 16.1 %collective-permute-start.6 = (f32[128,128]{1,0:T(8,128)S(1)}, f32[128,128]{1,0:T(8,128)S(1)}, u32[]{:S(2)}, u32[]{:S(2)}) collective-permute-start(f32[128,128]{1,0:T(8,128)S(1)} %collective-permute-done.3.t0), channel_id=1, source_target_pairs={{0,12},{4,0},{8,4},{12,8},{1,13},{5,1},{9,5},{13,9},{2,14},{6,2},{... | collective-permute-start | bytes 196616 | tf_op jit(solution)/shard_map/ppermute | solution.py:27
  16.9 32.1 %collective-permute-start.8 = (f32[264,128]{1,0:T(8,128)S(1)}, f32[264,128]{1,0:T(8,128)S(1)}, u32[]{:S(2)}, u32[]{:S(2)}) collective-permute-start(f32[264,128]{1,0:T(8,128)S(1)} %both.1.s0), channel_id=1, source_target_pairs={{0,2},{1,3},{2,0},{3,1},{4,6},{5,7},{6,4},{7,5},{8,10},{9,11},{10,... | collective-permute-start | bytes 405512 | tf_op jit(solution)/shard_map/ppermute | solution.py:35
  21.9 3.6 %collective-permute-start = (s32[1,128]{1,0:T(1,128)S(1)}, s32[1,128]{1,0:T(1,128)S(1)}, u32[]{:S(2)}, u32[]{:S(2)}) collective-permute-start(s32[1,128]{1,0:T(1,128)S(1)} %bitcast.28), channel_id=1, source_target_pairs={{0,64},{64,128},{128,192},{192,0},{1,65},{65,129},{129,193},{193,1... | collective-permute-start | bytes 1544 | tf_op jit(solution)/shard_map/ppermute | solution.py:31
  25.6 3.9 %collective-permute-start.1 = (s32[1,128]{1,0:T(1,128)S(1)}, s32[1,128]{1,0:T(1,128)S(1)}, u32[]{:S(2)}, u32[]{:S(2)}) collective-permute-start(s32[1,128]{1,0:T(1,128)S(1)} %bitcast.29), channel_id=1, source_target_pairs={{0,128},{64,192},{128,0},{192,64},{1,129},{65,193},{129,1},{193,65... | collective-permute-start | bytes 1544 | tf_op jit(solution)/shard_map/ppermute | solution.py:31
  29.5 2.4 %collective-permute-start.2 = (s32[1,128]{1,0:T(1,128)S(1)}, s32[1,128]{1,0:T(1,128)S(1)}, u32[]{:S(2)}, u32[]{:S(2)}) collective-permute-start(s32[1,128]{1,0:T(1,128)S(1)} %bitcast.30), channel_id=1, source_target_pairs={{0,192},{64,0},{128,64},{192,128},{1,193},{65,1},{129,65},{193,129... | collective-permute-start | bytes 1544 | tf_op jit(solution)/shard_map/ppermute | solution.py:31

commit v7 on v6

--- a/solution.py
+++ b/solution.py
@@ -66,8 +66,8 @@
     return band >> 4, lev, (lax.axis_index("y") - band) & 3, row
 
 
-def prepare_kernel(source_ref, taper_ref, thick_ref, scalars_ref):
-    source = source_ref[...]
+def prepare_kernel(packed_ref, scalars_ref):
+    source = packed_ref[0:1, :].astype(jnp.int32)
     x, lev, table, _ = parts_of(source)
     holder = (x * 4 + lev) * 4 + table
     member = iota((64, ROW), 0) == holder
@@ -76,7 +76,7 @@
     rank = jnp.sum(jnp.where(member, count, 0.0), axis=0, keepdims=True)
     pos = holder * 2 + rank.astype(jnp.int32)
 
-    taper, thick = taper_ref[...], thick_ref[...]
+    taper, thick = packed_ref[1:2, :], packed_ref[2:3, :]
     levels = taper.shape[1]
     diagonal = iota((LEVELS, levels), 0) == iota((LEVELS, levels), 1)
 
@@ -206,13 +206,16 @@
     table = along_z(pattern)
     source = block_source.reshape(1, ROW)
     asked = [along_x(source, k) for k in (1, 2, 3)]
+    room = (0, ROW - levels)
+    packed = jnp.stack([block_source.astype(f32), jnp.pad(taper, room), jnp.pad(thickness, room)])
     scalars = pl.pallas_call(
         prepare_kernel,
         out_shape=jax.ShapeDtypeStruct((2 * LEVELS + 24, ROW), f32),
-        in_specs=[vmem] * 3,
-        out_specs=vmem,
+        in_specs=[vmem],
+        out_specs=vmem,
+        compiler_params=pltpu.CompilerParams(vmem_limit_bytes=4 << 20),
         name="prepare",
-    )(source, taper.reshape(1, levels), thickness.reshape(1, levels))
+    )(packed)
     tables = [table] + [along_y(table, k) for k in (1, 2, 3)]
     wanted = pl.pallas_call(
         wanted_kernel,

time: 49.9 us -> 49.1 us (0.984)
  Pallas kernels: 8.69 us -> 7.34 us
  other arithmetic: 0 us -> 0.72 us
    pallas_call x1, Pallas kernels: 1.5 us -> 0.16 us  [program(): pl.pallas_call(prepare_kernel, out_shape=jax.ShapeDtypeStruct((2 * LEVELS...]
    unnamed x6 -> x4, local copies, waits for them, and re-layouts: 0.82 us -> 0.01 us
    another operation x0 -> x2, other arithmetic: none -> 0.72 us  [program(): jnp.stack([block_source.astype(f32), jnp.pad(taper, room), jnp.pad(thickn...]
    another operation x0 -> x1, local copies, waits for them, and re-layouts: none -> 0.67 us  [program(): jnp.stack([block_source.astype(f32), jnp.pad(taper, room), jnp.pad(thickn...]
where the time goes in v7:
time: 49.1 us; the launch traced here: 48.9 us
  starting transfers between devices  17 us (35%)
  blocking collectives  13.1 us (27%)
  waiting for transfers between devices  9.33 us (19%)
  Pallas kernels  7.34 us (15%)
  other arithmetic  0.72 us (1%)
  between operations  0.72 us (1%)
  local copies, waits for them, and re-layouts  0.68 us (1%)
    all_to_all x1, blocking collectives, program(): lax.all_to_all(picked.reshape(16, 8, ROW), ('x', 'lev'), 0, 0, tiled=True)  13.1 us
    ppermute x2, starting transfers between devices, across_lev(): return lax.ppermute(a, 'lev', [(i, i ^ flip) for i in range(4)])  5.82 us
    ppermute x3, waiting for transfers between devices, along_x(): return lax.ppermute(a, 'x', [(x, (x + step) % 4) for x in range(4)])  5.37 us
    ppermute x3, starting transfers between devices, along_y(): return lax.ppermute(a, 'y', [(y, (y + step) % 4) for y in range(4)])  4.7 us
    ppermute x3, starting transfers between devices, along_x(): return lax.ppermute(a, 'x', [(x, (x + step) % 4) for x in range(4)])  4.6 us
    ppermute x1, waiting for transfers between devices, along_z(): return lax.ppermute(a, ('z', 'lev'), pairs)  3.95 us
    pallas_call x1, Pallas kernels, program(): pl.pallas_call(perturb_kernel, out_shape=(jax.ShapeDtypeStruct(x.shape, x...  3.39 us
    pallas_call x1, Pallas kernels, program(): pl.pallas_call(column_kernel, out_shape=(jax.ShapeDtypeStruct((2 * ROW +...  2.55 us
  transfers between devices with their start and end apart: 9, of which 4 were waited for; matrix products, arithmetic and copies ran while one was open for 0% of the time, Pallas kernels for 8%

profile of v7, /device:TPU:65, one launch (start us, length us, event | category | flops | bytes accessed | tf_op | source)
XLA Modules:
  0.0 48.9 jit_solution(1812903877461428439)
XLA Ops:
  0.6 0.0 copy-start.1
  0.6 0.0 copy-start
  0.6 0.7 %convert_bitcast_fusion = f32[1,128]{1,0:T(1,128)S(1)} fusion(s32[128]{0:T(128)} %param.8), kind=kLoop, calls=%fused_computation.3 | loop fusion | flops 128 | bytes 1024 | tf_op jit(solution)/shard_map/stack | solution.py:210
  1.4 0.7 %pad_bitcast_fusion = (f32[1,128]{1,0:T(1,128)S(1)}, f32[1,128]{1,0:T(1,128)S(1)}) fusion(f32[34]{0:T(128)} %param.7, f32[34]{0:T(128)} %param.6), kind=kLoop, calls=%fused_computation.1 | loop fusion | bytes 1296 | tf_op jit(solution)/shard_map/stack | solution.py:210
  2.0 0.2 prepare.1.scalars_ref
  2.2 2.5 %columns.1 = (f32[264,128]{1,0:T(8,128)S(1)}, bf16[512,128]{1,0:T(8,128)(2,1)S(1)}, bf16[22,512,128]{2,1,0:T(8,128)(2,1)S(1)}) custom-call(f32[104,128]{1,0:T(8,128)S(1)} %prepare.1.scalars_ref, bf16[34,512,128]{2,1,0:T(8,128)(2,1)} %bitcast.26), custom_call_target="tpu_custom_call" | custom-call | flops 10000000 | bytes 4500000 | tf_op jit(solution)/shard_map/columns/pallas_call | solution.py:230
  4.8 0.8 %collective-permute-start.7 = (f32[264,128]{1,0:T(8,128)S(1)}, f32[264,128]{1,0:T(8,128)S(1)}, u32[]{:S(2)}, u32[]{:S(2)}) collective-permute-start(f32[264,128]{1,0:T(8,128)S(1)} %get-tuple-element.11.a_ref), channel_id=1, source_target_pairs={{0,1},{1,0},{2,3},{3,2},{4,5},{5,4},{6,7},{7,6},{8,9},{9,8},{10,11... | collective-permute-start | bytes 405512 | tf_op jit(solution)/shard_map/ppermute | solution.py:35
  5.5 0.0 copy-done
  5.5 1.9 %collective-permute-start.3 = (f32[128,128]{1,0:T(8,128)S(1)}, f32[128,128]{1,0:T(8,128)S(1)}, u32[]{:S(2)}, u32[]{:S(2)}) collective-permute-start(f32[128,128]{1,0:T(8,128)S(1)} %copy-done), channel_id=1, source_target_pairs={{0,0},{50,1},{17,2},{35,3},{16,16},{2,17},{33,18},{51,19},{32,32},... | collective-permute-start | bytes 196616 | tf_op jit(solution)/shard_map/ppermute | solution.py:23
  7.4 3.9 %collective-permute-done.3.t0 = f32[128,128]{1,0:T(8,128)S(1)} collective-permute-done((f32[128,128]{1,0:T(8,128)S(1)}, f32[128,128]{1,0:T(8,128)S(1)}, u32[]{:S(2)}, u32[]{:S(2)}) %collective-permute-start.3) | collective-permute-done | bytes 65568 | tf_op jit(solution)/shard_map/ppermute | solution.py:23
  11.4 1.0 %collective-permute-start.4 = (f32[128,128]{1,0:T(8,128)S(1)}, f32[128,128]{1,0:T(8,128)S(1)}, u32[]{:S(2)}, u32[]{:S(2)}) collective-permute-start(f32[128,128]{1,0:T(8,128)S(1)} %collective-permute-done.3.t0), channel_id=1, source_target_pairs={{0,4},{4,8},{8,12},{12,0},{1,5},{5,9},{9,13},{13,1},{2,6},{6,10},{... | collective-permute-start | bytes 196616 | tf_op jit(solution)/shard_map/ppermute | solution.py:27
  12.4 2.9 %collective-permute-start.5 = (f32[128,128]{1,0:T(8,128)S(1)}, f32[128,128]{1,0:T(8,128)S(1)}, u32[]{:S(2)}, u32[]{:S(2)}) collective-permute-start(f32[128,128]{1,0:T(8,128)S(1)} %collective-permute-done.3.t0), channel_id=1, source_target_pairs={{0,8},{4,12},{8,0},{12,4},{1,9},{5,13},{9,1},{13,5},{2,10},{6,14},... | collective-permute-start | bytes 196616 | tf_op jit(solution)/shard_map/ppermute | solution.py:27
  15.3 0.8 %collective-permute-start.6 = (f32[128,128]{1,0:T(8,128)S(1)}, f32[128,128]{1,0:T(8,128)S(1)}, u32[]{:S(2)}, u32[]{:S(2)}) collective-permute-start(f32[128,128]{1,0:T(8,128)S(1)} %collective-permute-done.3.t0), channel_id=1, source_target_pairs={{0,12},{4,0},{8,4},{12,8},{1,13},{5,1},{9,5},{13,9},{2,14},{6,2},{... | collective-permute-start | bytes 196616 | tf_op jit(solution)/shard_map/ppermute | solution.py:27
  16.1 0.0 collective-permute-done.7.b_ref
  16.1 5.1 %collective-permute-start.8 = (f32[264,128]{1,0:T(8,128)S(1)}, f32[264,128]{1,0:T(8,128)S(1)}, u32[]{:S(2)}, u32[]{:S(2)}) collective-permute-start(f32[264,128]{1,0:T(8,128)S(1)} %both.1.s0), channel_id=1, source_target_pairs={{0,2},{1,3},{2,0},{3,1},{4,6},{5,7},{6,4},{7,5},{8,10},{9,11},{10,... | collective-permute-start | bytes 405512 | tf_op jit(solution)/shard_map/ppermute | solution.py:35
  21.2 0.0 copy-done.1
  21.2 1.2 %collective-permute-start = (s32[1,128]{1,0:T(1,128)S(1)}, s32[1,128]{1,0:T(1,128)S(1)}, u32[]{:S(2)}, u32[]{:S(2)}) collective-permute-start(s32[1,128]{1,0:T(1,128)S(1)} %bitcast.30), channel_id=1, source_target_pairs={{0,64},{64,128},{128,192},{192,0},{1,65},{65,129},{129,193},{193,1... | collective-permute-start | bytes 1544 | tf_op jit(solution)/shard_map/ppermute | solution.py:31
  22.4 2.4 %collective-permute-done.from1 = s32[1,128]{1,0:T(1,128)S(1)} collective-permute-done((s32[1,128]{1,0:T(1,128)S(1)}, s32[1,128]{1,0:T(1,128)S(1)}, u32[]{:S(2)}, u32[]{:S(2)}) %collective-permute-start) | collective-permute-done | bytes 544 | tf_op jit(solution)/shard_map/ppermute | solution.py:31
  24.8 1.8 %collective-permute-start.1 = (s32[1,128]{1,0:T(1,128)S(1)}, s32[1,128]{1,0:T(1,128)S(1)}, u32[]{:S(2)}, u32[]{:S(2)}) collective-permute-start(s32[1,128]{1,0:T(1,128)S(1)} %bitcast.31), channel_id=1, source_target_pairs={{0,128},{64,192},{128,0},{192,64},{1,129},{65,193},{129,1},{193,65... | collective-permute-start | bytes 1544 | tf_op jit(solution)/shard_map/ppermute | solution.py:31
  26.6 2.1 %collective-permute-done.1.from2 = s32[1,128]{1,0:T(1,128)S(1)} collective-permute-done((s32[1,128]{1,0:T(1,128)S(1)}, s32[1,128]{1,0:T(1,128)S(1)}, u32[]{:S(2)}, u32[]{:S(2)}) %collective-permute-start.1) | collective-permute-done | bytes 544 | tf_op jit(solution)/shard_map/ppermute | solution.py:31
  28.7 1.6 %collective-permute-start.2 = (s32[1,128]{1,0:T(1,128)S(1)}, s32[1,128]{1,0:T(1,128)S(1)}, u32[]{:S(2)}, u32[]{:S(2)}) collective-permute-start(s32[1,128]{1,0:T(1,128)S(1)} %bitcast.32), channel_id=1, source_target_pairs={{0,192},{64,0},{128,64},{192,128},{1,193},{65,1},{129,65},{193,129... | collective-permute-start | bytes 1544 | tf_op jit(solution)/shard_map/ppermute | solution.py:31
  30.3 0.9 %collective-permute-done.2.from3 = s32[1,128]{1,0:T(1,128)S(1)} collective-permute-done((s32[1,128]{1,0:T(1,128)S(1)}, s32[1,128]{1,0:T(1,128)S(1)}, u32[]{:S(2)}, u32[]{:S(2)}) %collective-permute-start.2) | collective-permute-done | bytes 544 | tf_op jit(solution)/shard_map/ppermute | solution.py:31
  31.1 0.3 wanted.1.ids_ref
  31.4 0.0 collective-permute-done.4.t1
  31.4 0.0 collective-permute-done.5.t2
  31.4 0.0 collective-permute-done.6.t3
  31.4 0.3 pick.1
  31.7 13.1 %all_to_all.5 = f32[16,8,128]{2,1,0:T(8,128)S(1)} all-to-all(f32[16,8,128]{2,1,0:T(8,128)S(1)} %bitcast.25), channel_id=1, replica_groups=mesh['x'=4,'z'=4,'y'=4,'lev'=4] {'x','lev'}, dimensions={0} | all-to-all | bytes 131072 | tf_op jit(solution)/shard_map/all_to_all | solution.py:268
  44.8 3.4 %perturb.1 = (bf16[34,512,128]{2,1,0:T(8,128)(2,1)}, f32[128,128]{1,0:T(8,128)S(1)}) custom-call(f32[104,128]{1,0:T(8,128)S(1)} %prepare.1.scalars_ref, f32[128,128]{1,0:T(8,128)S(1)} %bitcast.24, bf16[512,128]{1,0:T(8,128)(2,1)S(1)} %get-tuple-element.7.place_ref, bf16[22,512,128]{2,1,0:T(8,128)(2,1)S(1)} %get-tuple-element.8.head_ref, ...), custom_call_target="tpu_custom_call" | custom-call | flops 10000000 | bytes 9000000 | tf_op jit(solution)/shard_map/perturb/pallas_call | solution.py:270
  48.2 0.0 collective-permute-done.8.s1
  48.2 0.7 %integrals.1 = f32[256,128]{1,0:T(8,128)} custom-call(f32[128,128]{1,0:T(8,128)S(1)} %get-tuple-element.10.local_ref, f32[264,128]{1,0:T(8,128)S(1)} %both.1.s0, f32[264,128]{1,0:T(8,128)S(1)} %collective-permute-done.8.s1), custom_call_target="tpu_custom_call" | custom-call | tf_op jit(solution)/shard_map/integrals/pallas_call | solution.py:286
  (2 shorter events, 0.0 us)
Async XLA Ops:
  0.6 20.5 %copy-start.1 = (s32[128]{0:T(128)S(1)}, s32[128]{0:T(128)}, u32[]{:S(2)}) copy-start(s32[128]{0:T(128)} %param.8) | copy-start | bytes 1540
  0.6 4.9 %copy-start = (f32[128,128]{1,0:T(8,128)S(1)}, f32[128,128]{1,0:T(8,128)}, u32[]{:S(2)}) copy-start(f32[128,128]{1,0:T(8,128)} %param.5) | copy-start | bytes 196612
  4.8 11.3 %collective-permute-start.7 = (f32[264,128]{1,0:T(8,128)S(1)}, f32[264,128]{1,0:T(8,128)S(1)}, u32[]{:S(2)}, u32[]{:S(2)}) collective-permute-start(f32[264,128]{1,0:T(8,128)S(1)} %get-tuple-element.11.a_ref), channel_id=1, source_target_pairs={{0,1},{1,0},{2,3},{3,2},{4,5},{5,4},{6,7},{7,6},{8,9},{9,8},{10,11... | collective-permute-start | bytes 405512 | tf_op jit(solution)/shard_map/ppermute | solution.py:35
  5.5 5.9 %collective-permute-start.3 = (f32[128,128]{1,0:T(8,128)S(1)}, f32[128,128]{1,0:T(8,128)S(1)}, u32[]{:S(2)}, u32[]{:S(2)}) collective-permute-start(f32[128,128]{1,0:T(8,128)S(1)} %copy-done), channel_id=1, source_target_pairs={{0,0},{50,1},{17,2},{35,3},{16,16},{2,17},{33,18},{51,19},{32,32},... | collective-permute-start | bytes 196616 | tf_op jit(solution)/shard_map/ppermute | solution.py:23
  11.4 20.0 %collective-permute-start.4 = (f32[128,128]{1,0:T(8,128)S(1)}, f32[128,128]{1,0:T(8,128)S(1)}, u32[]{:S(2)}, u32[]{:S(2)}) collective-permute-start(f32[128,128]{1,0:T(8,128)S(1)} %collective-permute-done.3.t0), channel_id=1, source_target_pairs={{0,4},{4,8},{8,12},{12,0},{1,5},{5,9},{9,13},{13,1},{2,6},{6,10},{... | collective-permute-start | bytes 196616 | tf_op jit(solution)/shard_map/ppermute | solution.py:27
  12.4 19.0 %collective-permute-start.5 = (f32[128,128]{1,0:T(8,128)S(1)}, f32[128,128]{1,0:T(8,128)S(1)}, u32[]{:S(2)}, u32[]{:S(2)}) collective-permute-start(f32[128,128]{1,0:T(8,128)S(1)} %collective-permute-done.3.t0), channel_id=1, source_target_pairs={{0,8},{4,12},{8,0},{12,4},{1,9},{5,13},{9,1},{13,5},{2,10},{6,14},... | collective-permute-start | bytes 196616 | tf_op jit(solution)/shard_map/ppermute | solution.py:27
  15.3 16.1 %collective-permute-start.6 = (f32[128,128]{1,0:T(8,128)S(1)}, f32[128,128]{1,0:T(8,128)S(1)}, u32[]{:S(2)}, u32[]{:S(2)}) collective-permute-start(f32[128,128]{1,0:T(8,128)S(1)} %collective-permute-done.3.t0), channel_id=1, source_target_pairs={{0,12},{4,0},{8,4},{12,8},{1,13},{5,1},{9,5},{13,9},{2,14},{6,2},{... | collective-permute-start | bytes 196616 | tf_op jit(solution)/shard_map/ppermute | solution.py:27
  16.1 32.1 %collective-permute-start.8 = (f32[264,128]{1,0:T(8,128)S(1)}, f32[264,128]{1,0:T(8,128)S(1)}, u32[]{:S(2)}, u32[]{:S(2)}) collective-permute-start(f32[264,128]{1,0:T(8,128)S(1)} %both.1.s0), channel_id=1, source_target_pairs={{0,2},{1,3},{2,0},{3,1},{4,6},{5,7},{6,4},{7,5},{8,10},{9,11},{10,... | collective-permute-start | bytes 405512 | tf_op jit(solution)/shard_map/ppermute | solution.py:35
  21.2 3.6 %collective-permute-start = (s32[1,128]{1,0:T(1,128)S(1)}, s32[1,128]{1,0:T(1,128)S(1)}, u32[]{:S(2)}, u32[]{:S(2)}) collective-permute-start(s32[1,128]{1,0:T(1,128)S(1)} %bitcast.30), channel_id=1, source_target_pairs={{0,64},{64,128},{128,192},{192,0},{1,65},{65,129},{129,193},{193,1... | collective-permute-start | bytes 1544 | tf_op jit(solution)/shard_map/ppermute | solution.py:31
  24.8 3.9 %collective-permute-start.1 = (s32[1,128]{1,0:T(1,128)S(1)}, s32[1,128]{1,0:T(1,128)S(1)}, u32[]{:S(2)}, u32[]{:S(2)}) collective-permute-start(s32[1,128]{1,0:T(1,128)S(1)} %bitcast.31), channel_id=1, source_target_pairs={{0,128},{64,192},{128,0},{192,64},{1,129},{65,193},{129,1},{193,65... | collective-permute-start | bytes 1544 | tf_op jit(solution)/shard_map/ppermute | solution.py:31
  28.7 2.4 %collective-permute-start.2 = (s32[1,128]{1,0:T(1,128)S(1)}, s32[1,128]{1,0:T(1,128)S(1)}, u32[]{:S(2)}, u32[]{:S(2)}) collective-permute-start(s32[1,128]{1,0:T(1,128)S(1)} %bitcast.32), channel_id=1, source_target_pairs={{0,192},{64,0},{128,64},{192,128},{1,193},{65,1},{129,65},{193,129... | collective-permute-start | bytes 1544 | tf_op jit(solution)/shard_map/ppermute | solution.py:31
